TPU v7x, 32 devices: a whole 2x2x4 slice. The times are simulated.
32 devices in a mesh: row: 4 (over y, core), col: 8 (over z, x).
Axes of the slice: x: 2, y: 2, z: 4, core: 2. Of those that a mesh axis runs over, the one named last changes fastest.
Arguments:
- right_side: float32 [32768], P(('row', 'col')), may hold values from -6 to 6
- eigen_basis: bfloat16 [12288, 512], P(('row', 'col')), may hold values from -0.0546875 to 0.0546875
- tile_left: bfloat16 [12288, 1024], P('row', 'col'), may hold values from -0.4375 to 0.4375
- tile_right: bfloat16 [512, 12288], P('row', 'col'), may hold values from -0.625 to 0.625
- piece_owner: int32 [4, 1024], P('row', 'col'), may hold values from 0 to 32767
- omega_main: float32 [512, 512], replicated, may hold values from 0 to 1
- damping: float32 [512], replicated, may hold values from 0.05 to 1
- local_basis: bfloat16 [256, 256, 256], P(('row', 'col')), may hold values from -0.375 to 0.375
- local_omega: float32 [256, 256, 256], P(('row', 'col')), may hold values from 0 to 1
- local_left: bfloat16 [256, 256, 256], P(('row', 'col')), may hold values from -0.75 to 0.75
- local_right: bfloat16 [256, 256, 256], P(('row', 'col')), may hold values from -0.75 to 0.75
- local_owner: int32 [256, 256], P(('row', 'col')), may hold values from 0 to 32767
Outputs:
- solution: float32 [32768], P(('row', 'col'))
- residual: float32 [32768], P(('row', 'col'))
All inputs are finite; a program needn't handle non-finite values.
Results may differ from a plain program's by a relative error of at most 0.00057.
Values may be sent and summed in bfloat16 or wider, within the bound.
No kernel may reach another device: no remote copies, remote signals or barrier semaphores. Data moves between devices by JAX's collectives and lax.ppermute only.
A program may use at most 128 MiB of HBM per device.

v0:
```python
import jax
import jax.numpy as jnp
from jax import lax
from jax.sharding import PartitionSpec as P

ITERS = 2


precise = lax.Precision.HIGHEST
contract = (((0,), (0,)), ((), ()))


def squared_sum(vector):
    return lax.psum(jnp.sum(vector * vector), ("row", "col"))


def local(
    right_side,
    eigen_basis,
    tile_left,
    tile_right,
    piece_owner,
    omega_main,
    damping,
    local_basis,
    local_omega,
    local_left,
    local_right,
    local_owner,
):
    basis_rows = lax.all_gather(eigen_basis, "col", axis=0, tiled=True)
    basis_cols = lax.all_gather(eigen_basis, "row", axis=0, tiled=True)
    left_proj = lax.dot_general(
        tile_left, basis_rows, contract, preferred_element_type=jnp.float32
    ).astype(jnp.bfloat16)
    right_proj = jnp.dot(tile_right, basis_cols, preferred_element_type=jnp.float32).astype(
        jnp.bfloat16
    )
    left_pf = left_proj.astype(jnp.float32)
    right_pf = right_proj.astype(jnp.float32)
    local_lp = jnp.einsum(
        "lps,lsk->lpk", local_left, local_basis, preferred_element_type=jnp.float32
    ).astype(jnp.bfloat16)
    local_rp = jnp.einsum(
        "lps,lsk->lpk", local_right, local_basis, preferred_element_type=jnp.float32
    ).astype(jnp.bfloat16)
    left_float = local_lp.astype(jnp.float32)
    right_float = local_rp.astype(jnp.float32)
    owners = piece_owner[0]
    local_flat = local_owner.reshape(-1)
    omega_sym = 0.5 * (omega_main + omega_main.T)
    local_sym = 0.5 * (local_omega + jnp.swapaxes(local_omega, 1, 2))
    solution = jnp.zeros_like(right_side)
    residual = right_side
    direction = right_side
    norm_now = squared_sum(residual)
    for counter in range(ITERS):
        all_duals = lax.all_gather(direction, ("row", "col"), axis=0, tiled=True)
        coeffs = all_duals[owners]
        scaled_right = (coeffs[:, None] * right_pf).astype(jnp.bfloat16)
        scaled_left = (coeffs[:, None] * left_pf).astype(jnp.bfloat16)
        row_terms = jnp.dot(tile_left, scaled_right, preferred_element_type=jnp.float32)
        row_share = lax.psum_scatter(row_terms, "col", scatter_dimension=0, tiled=True)
        col_terms = lax.dot_general(
            tile_right, scaled_left, contract, preferred_element_type=jnp.float32
        )
        col_share = lax.psum_scatter(col_terms, "row", scatter_dimension=0, tiled=True)
        field_half = (row_share + col_share).astype(jnp.bfloat16)
        field_rows = lax.all_gather(field_half, "col", axis=0, tiled=True)
        field_cols = lax.all_gather(field_half, "row", axis=0, tiled=True)
        own_terms = lax.dot_general(
            basis_rows, field_rows, contract, preferred_element_type=jnp.float32
        )
        curvature = lax.psum(own_terms.astype(jnp.bfloat16), "row").astype(jnp.float32)
        weights = omega_sym * curvature
        left_field = lax.dot_general(
            tile_left, field_rows, contract, preferred_element_type=jnp.float32
        )
        right_field = jnp.dot(tile_right, field_cols, preferred_element_type=jnp.float32)
        left_rest = left_field - jnp.dot(left_pf, curvature, precision=precise)
        right_rest = right_field - jnp.dot(right_pf, curvature, precision=precise)
        weighted = jnp.dot(right_pf, weights, precision=precise)
        inner_sum = (
            left_pf * weighted + left_rest * (damping * right_pf) + damping * left_pf * right_rest
        )
        big_values = 2.0 * jnp.sum(inner_sum, axis=1)
        local_coeffs = all_duals[local_owner]
        scaled = local_coeffs[:, :, None] * left_float
        half_t = jnp.einsum("lpa,lpb->lab", scaled, right_float, precision=precise)
        gram_mat = half_t + jnp.swapaxes(half_t, 1, 2)
        local_w = local_sym * gram_mat
        mixed_rows = jnp.einsum("lpb,lba->lpa", right_float, local_w, precision=precise)
        local_values = 2.0 * jnp.sum(left_float * mixed_rows, axis=2)
        totals = jnp.zeros((all_duals.shape[0],), jnp.float32).at[owners].add(big_values)
        totals = totals.at[local_flat].add(local_values.reshape(-1))
        returned = lax.psum_scatter(totals, ("row", "col"), scatter_dimension=0, tiled=True)
        applied = direction + returned
        step_size = norm_now / lax.psum(jnp.sum(direction * applied), ("row", "col"))
        solution = solution + step_size * direction
        residual = residual - step_size * applied
        norm_next = squared_sum(residual)
        direction = residual + norm_next / norm_now * direction
        norm_now = norm_next
    return (solution, residual)


def solution(mesh):
    placed = (
        P(("row", "col")),
        P(("row", "col"), None),
        P("row", "col"),
        P("row", "col"),
        P("row", "col"),
        P(),
        P(),
        P(("row", "col"), None, None),
        P(("row", "col"), None, None),
        P(("row", "col"), None, None),
        P(("row", "col"), None, None),
        P(("row", "col"), None),
    )
    return jax.shard_map(
        local,
        mesh=mesh,
        in_specs=placed,
        out_specs=(P(("row", "col")), P(("row", "col"))),
        check_vma=False,
    )
```

profile of v0, /device:TPU:0, one launch (start us, length us, event | category | flops | bytes accessed | tf_op | source)
XLA Modules:
  0.0 1149.6 jit_solution(4164054287538820386)
XLA Ops:
  8.7 72.8 %all_gather.26 = f32[32768]{0:T(1024)S(1)} all-gather(f32[1024]{0:T(1024)} %param.12), channel_id=1, replica_groups=mesh['row'=4,'col'=8] {'row','col'}, dimensions={0}, use_global_device_ids=true | all-gather | bytes 135168 | tf_op jit(solution)/shard_map/all_gather | solution.py:58
  83.4 2.8 convolution_convert_fusion.5
  86.2 2.3 convolution_bitcast_fusion.3
  88.6 5.5 all-gather.9.cloned.1.call-done
  94.1 1.8 convolution_convert_fusion.4
  95.9 3.7 convolution_bitcast_fusion.1
  99.7 34.7 %reduce-scatter.7.cloned.1.call-done = f32[384,512]{0,1:T(8,128)} async-done(((f32[1536,512]{0,1:T(8,128)}), f32[384,512]{0,1:T(8,128)}) %reduce-scatter.7.cloned.1.call-update) | async-done | bytes 786448 | tf_op jit(solution)/shard_map/reduce_scatter | solution.py:67
  134.4 121.5 %reduce-scatter.5.cloned.1.call-done = f32[384,512]{0,1:T(8,128)} async-done(((f32[3072,512]{0,1:T(8,128)}), f32[384,512]{0,1:T(8,128)}) %reduce-scatter.5.cloned.1.call-update) | async-done | bytes 786448 | tf_op jit(solution)/shard_map/reduce_scatter | solution.py:63
  255.9 2.2 add_convert_fusion.1
  258.7 1.3 copy.36
  260.1 11.8 %gather_fusion.1 = f32[2048]{0:T(1024)S(1)} fusion(f32[32768]{0:T(1024)S(1)} %all_gather.26, s32[2048]{0:T(1024)S(1)} %broadcast_clamp_fusion), kind=kCustom, calls=%fused_computation.1 | custom fusion | bytes 24576 | tf_op jit(solution)/shard_map/gather | solution.py:87
  273.7 2.6 fusion
  276.3 2.9 copy.41
  279.2 2.9 copy.40
  282.1 5.4 fusion.1
  288.2 2.8 convolution_bitcast_fusion.6
  291.0 50.8 %all-gather.11.cloned.1.call-done = bf16[3072,512]{0,1:T(8,128)(2,1)} async-done(((bf16[384,512]{0,1:T(8,128)(2,1)}), bf16[3072,512]{0,1:T(8,128)(2,1)}) %all-gather.11.cloned.1.call-update) | async-done | bytes 3145744 | tf_op jit(solution)/shard_map/all_gather | solution.py:69
  341.7 5.4 fusion.11
  347.4 3.9 convolution_bitcast_fusion.7
  351.4 27.6 %all-reduce.8.cloned.1.call-done = bf16[512,512]{0,1:T(8,128)(2,1)} async-done(((bf16[512,512]{0,1:T(8,128)(2,1)}), bf16[512,512]{0,1:T(8,128)(2,1)}) %all-reduce.8.cloned.1.call-update) | async-done | bytes 524304 | tf_op jit(solution)/shard_map/psum | solution.py:74
  379.0 2.6 convolution_multiply_fusion.1
  383.7 11.8 %scatter_fusion = f32[32768]{0:T(1024)S(1)} fusion(f32[32768]{0:T(1024)S(1)} %scatter_custom_fusion, s32[2048]{0:T(1024)S(1)} %bitcast.110, f32[2048]{0:T(1024)} %bitcast.113), kind=kCustom, calls=%fused_computation.5 | custom fusion | flops 2048 | bytes 32768 | tf_op jit(solution)/shard_map/scatter-add | solution.py:95
  396.2 124.7 %all-reduce.12.cloned.1.call-done = f32[32768]{0:T(1024)} async-done(((f32[32768]{0:T(1024)}), f32[32768]{0:T(1024)}) %all-reduce.12.cloned.1.call-update) | async-done | bytes 131088
  520.8 1.3 multiply_reduce_fusion.2
  522.2 39.5 %all-reduce.2 = (f32[]{:T(128)}, f32[]{:T(128)}) all-reduce(f32[]{:T(128)} %get-tuple-element.3, f32[]{:T(128)} %get-tuple-element.2), channel_id=1, replica_groups=mesh['row'=4,'col'=8] {'row','col'}, use_global_device_ids=true, to_apply=%region_1.0 | all-reduce | flops 2 | bytes 16 | tf_op jit(solution)/shard_map/psum | solution.py:14
  564.3 40.4 %psum.45 = f32[]{:T(128)} all-reduce(f32[]{:T(128)} %multiply_reduce_fusion.1), channel_id=1, replica_groups=mesh['row'=4,'col'=8] {'row','col'}, use_global_device_ids=true, to_apply=%region_13.0 | all-reduce | flops 1 | bytes 8 | tf_op jit(solution)/shard_map/psum | solution.py:14
  606.8 66.8 %all_gather.29 = f32[32768]{0:T(1024)S(1)} all-gather(f32[1024]{0:T(1024)S(1)} %multiply_add_fusion.1), channel_id=1, replica_groups=mesh['row'=4,'col'=8] {'row','col'}, dimensions={0}, use_global_device_ids=true | all-gather | bytes 135168 | tf_op jit(solution)/shard_map/all_gather | solution.py:58
  673.6 1.8 gather_fusion.2
  675.4 3.3 convolution_bitcast_fusion.2
  678.7 5.0 convolution_bitcast_fusion
  683.8 30.0 %reduce-scatter.11.cloned.1.call-done = f32[384,512]{0,1:T(8,128)} async-done(((f32[1536,512]{0,1:T(8,128)}), f32[384,512]{0,1:T(8,128)}) %reduce-scatter.11.cloned.1.call-update) | async-done | bytes 786448 | tf_op jit(solution)/shard_map/reduce_scatter | solution.py:67
  713.7 121.5 %reduce-scatter.9.cloned.1.call-done = f32[384,512]{0,1:T(8,128)} async-done(((f32[3072,512]{0,1:T(8,128)}), f32[384,512]{0,1:T(8,128)}) %reduce-scatter.9.cloned.1.call-update) | async-done | bytes 786448 | tf_op jit(solution)/shard_map/reduce_scatter | solution.py:63
  835.2 2.2 add_convert_fusion
  838.3 20.7 %gather_fusion.3 = f32[2048]{0:T(1024)} fusion(f32[32768]{0:T(1024)S(1)} %all_gather.29, s32[2048]{0:T(1024)} %copy-done.16), kind=kCustom, calls=%fused_computation.3 | custom fusion | bytes 24576 | tf_op jit(solution)/shard_map/gather | solution.py:87
  859.7 2.6 fusion.2
  862.2 2.9 copy.45
  865.1 5.7 fusion.3
  870.9 2.1 convolution_bitcast_fusion.4
  873.0 48.1 %all-gather.15.cloned.1.call-done = bf16[3072,512]{0,1:T(8,128)(2,1)} async-done(((bf16[384,512]{0,1:T(8,128)(2,1)}), bf16[3072,512]{0,1:T(8,128)(2,1)}) %all-gather.15.cloned.1.call-update) | async-done | bytes 3145744 | tf_op jit(solution)/shard_map/all_gather | solution.py:69
  921.1 5.4 fusion.12
  926.6 3.8 convolution_bitcast_fusion.5
  930.5 27.8 %all-reduce.10.cloned.1.call-done = bf16[512,512]{0,1:T(8,128)(2,1)} async-done(((bf16[512,512]{0,1:T(8,128)(2,1)}), bf16[512,512]{0,1:T(8,128)(2,1)}) %all-reduce.10.cloned.1.call-update) | async-done | bytes 524304 | tf_op jit(solution)/shard_map/psum | solution.py:74
  958.3 2.3 convolution_multiply_fusion
  961.3 1.4 scatter_custom_fusion.2
  962.7 11.6 %scatter_fusion.1 = f32[32768]{0:T(1024)S(1)} fusion(f32[32768]{0:T(1024)S(1)} %scatter_custom_fusion.2, s32[2048]{0:T(1024)S(1)} %bitcast.111, f32[2048]{0:T(1024)S(1)} %bitcast.112), kind=kCustom, calls=%fused_computation.7 | custom fusion | flops 2048 | bytes 32768 | tf_op jit(solution)/shard_map/scatter-add | solution.py:95
  975.0 124.7 %all-reduce.14.cloned.1.call-done = f32[32768]{0:T(1024)} async-done(((f32[32768]{0:T(1024)}), f32[32768]{0:T(1024)}) %all-reduce.14.cloned.1.call-update) | async-done | bytes 131088
  1101.0 39.4 %psum.47 = f32[]{:T(128)} all-reduce(f32[]{:T(128)} %multiply_reduce_fusion), channel_id=1, replica_groups=mesh['row'=4,'col'=8] {'row','col'}, use_global_device_ids=true, to_apply=%region_23.0 | all-reduce | flops 1 | bytes 8 | tf_op jit(solution)/shard_map/psum | solution.py:98
  1141.8 1.3 multiply_subtract_fusion
  (101 shorter events, 15.9 us)
Async XLA Ops:
  7.2 264.8 %copy-start = (bf16[8,256,256]{2,1,0:T(8,128)(2,1)S(1)}, bf16[8,256,256]{2,1,0:T(8,128)(2,1)}, u32[]{:S(2)}) copy-start(bf16[8,256,256]{2,1,0:T(8,128)(2,1)} %param.19) | copy-start | bytes 3145732
  7.2 76.2 %all-gather.7.cloned.1.call-start = ((), (), s32[]{:S(2)}) async-start(), calls=%async_computation.4 | async-start | bytes 3538944 | tf_op jit(solution)/shard_map/all_gather | solution.py:31
  7.9 86.2 %all-gather.9.cloned.1.call-start = ((), (), s32[]{:S(2)}) async-start(), calls=%async_computation.5 | async-start | bytes 1966080 | tf_op jit(solution)/shard_map/all_gather | solution.py:32
  8.7 125.7 %reduce-scatter.7.cloned.1.call-start = ((), (), s32[]{:S(2)}) async-start(), calls=%async_computation.7 | async-start | bytes 3932160 | tf_op jit(solution)/shard_map/reduce_scatter | solution.py:67
  82.2 300.2 %copy-start.21 = (s32[128]{0:T(128)}, s32[128]{0:T(128)S(1)}, u32[]{:S(2)}) copy-start(s32[128]{0:T(128)S(1)} %fusion.55) | copy-start | bytes 1540
  82.2 4.0 copy-start.20
  83.4 2.8 copy-start.5
  88.5 7.4 copy-start.3
  88.5 167.4 %reduce-scatter.5.cloned.1.call-start = ((), (), s32[]{:S(2)}) async-start(), calls=%async_computation.6 | async-start | bytes 7077888 | tf_op jit(solution)/shard_map/reduce_scatter | solution.py:63
  99.7 159.0 %copy-start.6 = (f32[512,512]{1,0:T(8,128)S(1)}, f32[512,512]{1,0:T(8,128)}, u32[]{:S(2)}) copy-start(f32[512,512]{1,0:T(8,128)} %param.17) | copy-start | bytes 3145732
  99.7 160.4 %copy-start.19 = (s32[8,256]{1,0:T(8,128)S(1)}, s32[8,256]{1,0:T(8,128)}, u32[]{:S(2)}) copy-start(s32[8,256]{1,0:T(8,128)} %param.23) | copy-start | bytes 24580
  99.7 188.5 %all-gather.13.cloned.1.call-start = ((), (), s32[]{:S(2)}) async-start(), calls=%async_computation.10 | async-start | bytes 1966080 | tf_op jit(solution)/shard_map/all_gather | solution.py:70
  258.1 83.6 %all-gather.11.cloned.1.call-start = ((), (), s32[]{:S(2)}) async-start(), calls=%async_computation.8 | async-start | bytes 3538944 | tf_op jit(solution)/shard_map/all_gather | solution.py:69
  258.7 120.3 %all-reduce.8.cloned.1.call-start = ((), (), s32[]{:S(2)}) async-start(), calls=%async_computation.9 | async-start | bytes 1048576 | tf_op jit(solution)/shard_map/psum | solution.py:74
  260.1 11.8 %copy-start.16 = (s32[2048]{0:T(1024)}, s32[2048]{0:T(1024)S(1)}, u32[]{:S(2)}) copy-start(s32[2048]{0:T(1024)S(1)} %broadcast_clamp_fusion) | copy-start | bytes 24580
  260.1 11.8 %copy-start.10 = (bf16[8,256,256]{2,1,0:T(8,128)(2,1)S(1)}, bf16[8,256,256]{2,1,0:T(8,128)(2,1)}, u32[]{:S(2)}) copy-start(bf16[8,256,256]{2,1,0:T(8,128)(2,1)} %param.22) | copy-start | bytes 3145732
  271.9 1.2 copy-start.11
  347.2 173.6 %all-reduce.12.cloned.1.call-start = ((), (), s32[]{:S(2)}) async-start(), calls=%async_computation.16 | async-start | bytes 262144
  351.4 30.2 %copy-start.17 = (f32[512]{0:T(512)S(1)}, f32[512]{0:T(512)}, u32[]{:S(2)}) copy-start(f32[512]{0:T(512)} %param.18) | copy-start | bytes 6148
  379.0 2.6 copy-start.9
  379.0 2.6 copy-start.14
  379.0 3.0 copy-start.12
  383.7 137.2 %copy-start.15 = (f32[1024]{0:T(1024)S(1)}, f32[1024]{0:T(1024)}, u32[]{:S(2)}) copy-start(f32[1024]{0:T(1024)} %param.12) | copy-start | bytes 12292
  395.4 0.6 copy-start.2
  396.1 317.6 %reduce-scatter.11.cloned.1.call-start = ((), (), s32[]{:S(2)}) async-start(), calls=%async_computation.12 | async-start | bytes 3932160 | tf_op jit(solution)/shard_map/reduce_scatter | solution.py:67
  678.7 156.6 %reduce-scatter.9.cloned.1.call-start = ((), (), s32[]{:S(2)}) async-start(), calls=%async_computation.11 | async-start | bytes 7077888 | tf_op jit(solution)/shard_map/reduce_scatter | solution.py:63
  683.7 187.1 %all-gather.17.cloned.1.call-start = ((), (), s32[]{:S(2)}) async-start(), calls=%async_computation.15 | async-start | bytes 1966080 | tf_op jit(solution)/shard_map/all_gather | solution.py:70
  837.5 83.6 %all-gather.15.cloned.1.call-start = ((), (), s32[]{:S(2)}) async-start(), calls=%async_computation.13 | async-start | bytes 3538944 | tf_op jit(solution)/shard_map/all_gather | solution.py:69
  838.0 120.3 %all-reduce.10.cloned.1.call-start = ((), (), s32[]{:S(2)}) async-start(), calls=%async_computation.14 | async-start | bytes 1048576 | tf_op jit(solution)/shard_map/psum | solution.py:74
  873.0 53.6 %copy-start.4 = (bf16[3072,128]{1,0:T(8,128)(2,1)S(1)}, bf16[3072,128]{1,0:T(8,128)(2,1)}, u32[]{:S(2)}) copy-start(bf16[3072,128]{1,0:T(8,128)(2,1)} %param.14) | copy-start | bytes 2359300
  926.6 31.7 %copy-start.7 = (f32[512,512]{1,0:T(8,128)S(1)}, f32[512,512]{1,0:T(8,128)}, u32[]{:S(2)}) copy-start(f32[512,512]{1,0:T(8,128)} %param.17) | copy-start | bytes 3145732
  926.6 173.2 %all-reduce.14.cloned.1.call-start = ((), (), s32[]{:S(2)}) async-start(), calls=%async_computation.17 | async-start | bytes 262144
  930.4 30.1 %copy-start.13 = (f32[128,512]{1,0:T(8,128)S(1)}, f32[128,512]{1,0:T(8,128)}, u32[]{:S(2)}) copy-start(f32[128,512]{1,0:T(8,128)} %convolution_bitcast_fusion.5) | copy-start | bytes 786436
  930.4 30.1 %copy-start.18 = (f32[512]{0:T(512)S(1)}, f32[512]{0:T(512)}, u32[]{:S(2)}) copy-start(f32[512]{0:T(512)} %param.18) | copy-start | bytes 6148
  958.3 2.3 copy-start.8
  974.3 0.7 copy-start.1
Sparse Core Ops, SparseCore 0:
  10.2 63.7 all-gather.6
  75.6 18.5 all-gather.8
  96.6 37.7 reduce-scatter.6
  137.8 117.9 reduce-scatter.4
  258.2 18.8 all-gather.12
  279.0 62.6 all-gather.10
  347.3 31.6 all-reduce.7
  396.2 124.5 all-reduce.11
  678.8 34.9 reduce-scatter.10
  717.2 118.0 reduce-scatter.8
  837.6 18.8 all-gather.16
  858.4 62.6 all-gather.14
  926.7 31.5 all-reduce.9
  975.1 124.5 all-reduce.13
where the time goes:
time: 1150 us
  waiting for transfers between devices  719 us (63%)
  blocking collectives  259 us (23%)
  matrix products  65.9 us (6%)
  local copies, waits for them, and re-layouts  48.9 us (4%)
  other arithmetic  37 us (3%)
  between operations  18.5 us (2%)
    unnamed x16, waiting for transfers between devices  252 us
    reduce_scatter x2, waiting for transfers between devices, local(): lax.psum_scatter(row_terms, 'col', scatter_dimension=0, tiled=True)  243 us
    all_gather x2, blocking collectives, local(): all_duals = lax.all_gather(direction, ('row', 'col'), axis=0, tiled=True)  140 us
    all_gather x2, waiting for transfers between devices, local(): field_rows = lax.all_gather(field_half, 'col', axis=0, tiled=True)  98.8 us
    psum x2, blocking collectives, squared_sum(): return lax.psum(jnp.sum(vector * vector), ('row', 'col'))  79.9 us
    reduce_scatter x2, waiting for transfers between devices, local(): lax.psum_scatter(col_terms, 'row', scatter_dimension=0, tiled=True)  64.6 us
    psum x2, waiting for transfers between devices, local(): lax.psum(own_terms.astype(jnp.bfloat16), 'row').astype(jnp.float32)  55.4 us
    psum x1, blocking collectives, local(): lax.psum(jnp.sum(direction * applied), ('row', 'col'))  39.4 us
  transfers between devices with their start and end apart: 14, of which 11 were waited for; matrix products, arithmetic and copies ran while one was open for 8% of the time, Pallas kernels for 0%

commit v1 on v0

v1 whole, which is shorter than its diff:
```python
import jax
import jax.numpy as jnp
from jax import lax
from jax.sharding import PartitionSpec as P

LANES = 128
BOTH = ("row", "col")
f32 = jnp.float32
bf16 = jnp.bfloat16


def tdot(a, b):
    return lax.dot_general(a, b, (((0,), (0,)), ((), ())), preferred_element_type=f32)


def mdot(a, b):
    return jnp.dot(a, b, preferred_element_type=f32)


def halves(x):
    top = lax.reduce_precision(x, 8, 7)
    return top.astype(bf16), (x - top).astype(bf16)


def onehot(index, size):
    return index[:, None] == lax.broadcasted_iota(jnp.int32, (index.shape[0], size), 1)


def spread(x, devices):
    return lax.all_to_all(jnp.broadcast_to(x[None], (devices,) + x.shape), BOTH, 0, 0, tiled=True)


def local(
    n_row,
    n_col,
    right_side,
    eigen_basis,
    tile_left,
    tile_right,
    piece_owner,
    omega_main,
    damping,
    local_basis,
    local_omega,
    local_left,
    local_right,
    local_owner,
):
    devices = n_row * n_col
    pieces = tile_left.shape[1]
    height, rank = eigen_basis.shape
    chunk = right_side.shape[0] // LANES
    heads = chunk * devices
    row_at = lax.axis_index("row")
    col_at = lax.axis_index("col")
    at = row_at * n_col + col_at

    basis_rows = lax.all_gather(eigen_basis, "col", axis=0, tiled=True)
    basis_cols = lax.all_gather(eigen_basis, "row", axis=0, tiled=True)
    own_words = jnp.concatenate(
        [right_side.reshape(chunk, LANES), piece_owner.reshape(-1, LANES).astype(f32)], axis=0
    )
    words = spread(own_words, devices)
    u_block = lax.all_to_all(tile_left.reshape(n_col, height, pieces), "col", 0, 0, tiled=True)
    u_block = jnp.swapaxes(u_block, 0, 1).reshape(height, n_col * pieces)
    v_block = jnp.swapaxes(tile_right.reshape(pieces, n_row, height), 0, 1)
    v_block = lax.all_to_all(v_block, "row", 0, 0, tiled=True).reshape(n_row * pieces, height)
    left_proj = tdot(tile_left, basis_rows).astype(bf16)
    right_proj = mdot(tile_right, basis_cols).astype(bf16)
    projs = lax.all_gather(
        jnp.concatenate([left_proj, right_proj], axis=1), BOTH, axis=0, tiled=True
    )
    left_all = projs[:, :rank]
    right_all = projs[:, rank:]
    right_group = lax.dynamic_slice_in_dim(right_all, row_at * n_col * pieces, n_col * pieces, 0)
    left_group = lax.dynamic_index_in_dim(
        left_all.reshape(n_row, n_col, pieces, rank), col_at, 1, keepdims=False
    ).reshape(n_row * pieces, rank)

    right_full = words[:, :chunk].reshape(heads, LANES)
    owners_all = words[:, chunk:].astype(jnp.int32).reshape(n_row, n_col, pieces)
    owners_u = lax.dynamic_index_in_dim(owners_all, row_at, 0, keepdims=False).reshape(-1)
    owners_v = lax.dynamic_index_in_dim(owners_all, col_at, 1, keepdims=False).reshape(-1)
    local_flat = local_owner.reshape(-1)
    owners_read = jnp.concatenate([owners_all.reshape(-1), local_flat])
    owners_write = jnp.concatenate([owners_u, owners_v, local_flat])
    read_head = onehot(owners_read // LANES, heads).astype(bf16)
    read_lane = onehot(owners_read % LANES, LANES)
    write_head = onehot(owners_write // LANES, heads).astype(bf16)
    write_lane = onehot(owners_write % LANES, LANES)

    omega_sym = 0.5 * (omega_main + omega_main.T)
    bend = damping[None, :] - 0.5 * omega_sym
    local_sym = 0.5 * (local_omega + jnp.swapaxes(local_omega, 1, 2))
    local_lp = jnp.einsum(
        "lps,lsk->lpk", local_left, local_basis, preferred_element_type=f32
    ).astype(bf16)
    local_rp = jnp.einsum(
        "lps,lsk->lpk", local_right, local_basis, preferred_element_type=f32
    ).astype(bf16)
    left_float = local_lp.astype(f32)

    def partial(vector):
        top, low = halves(vector)
        rows = mdot(read_head, jnp.concatenate([top, low], axis=1))
        rows = rows[:, :LANES] + rows[:, LANES:]
        coeffs = jnp.sum(jnp.where(read_lane, rows, 0.0), axis=1)
        coeffs_all = coeffs[: devices * pieces]
        grid = coeffs_all.reshape(n_row, n_col, pieces)
        coeffs_u = lax.dynamic_index_in_dim(grid, row_at, 0, keepdims=False).reshape(-1)
        coeffs_v = lax.dynamic_index_in_dim(grid, col_at, 1, keepdims=False).reshape(-1)
        local_coeffs = coeffs[devices * pieces :].reshape(local_owner.shape)

        half_k = tdot(left_all, (coeffs_all[:, None] * right_all.astype(f32)).astype(bf16))
        curvature = half_k + half_k.T
        scaled_right = (coeffs_u[:, None] * right_group.astype(f32)).astype(bf16)
        scaled_left = (coeffs_v[:, None] * left_group.astype(f32)).astype(bf16)
        field = mdot(u_block, scaled_right) + tdot(v_block, scaled_left)
        field = field.astype(bf16).astype(f32)
        bent_top, bent_low = halves(curvature * bend)
        pull = field * damping - (mdot(eigen_basis, bent_top) + mdot(eigen_basis, bent_low))
        pull_top, pull_low = halves(pull)
        back_u = tdot(u_block, pull_top) + tdot(u_block, pull_low)
        back_v = mdot(v_block, pull_top) + mdot(v_block, pull_low)
        values_u = 2.0 * jnp.sum(back_u * right_group.astype(f32), axis=1)
        values_v = 2.0 * jnp.sum(back_v * left_group.astype(f32), axis=1)

        scaled = (local_coeffs[:, :, None] * left_float).astype(bf16)
        half_t = jnp.einsum("lpa,lpb->lab", scaled, local_rp, preferred_element_type=f32)
        local_w = (local_sym * (half_t + jnp.swapaxes(half_t, 1, 2))).astype(bf16)
        mixed = jnp.einsum("lpb,lba->lpa", local_rp, local_w, preferred_element_type=f32)
        local_values = 2.0 * jnp.sum(left_float * mixed, axis=2)

        values = jnp.concatenate([values_u, values_v, local_values.reshape(-1)])
        top, low = halves(values)
        top = jnp.where(write_lane, top[:, None], jnp.zeros((), bf16))
        low = jnp.where(write_lane, low[:, None], jnp.zeros((), bf16))
        totals = tdot(write_head, jnp.concatenate([top, low], axis=1))
        return totals[:, :LANES] + totals[:, LANES:]

    def own(vector):
        return lax.dynamic_slice_in_dim(vector, at * chunk, chunk, 0)

    norm_now = jnp.sum(right_full * right_full)
    parts = partial(right_full).reshape(devices, chunk, LANES)
    share = jnp.sum(lax.all_to_all(parts, BOTH, 0, 0, tiled=True), axis=0)
    applied = right_full + spread(share, devices).reshape(heads, LANES)
    step_one = norm_now / jnp.sum(right_full * applied)
    residual = right_full - step_one * applied
    norm_next = jnp.sum(residual * residual)
    direction = residual + norm_next / norm_now * right_full
    totals = partial(direction)
    term = jnp.broadcast_to(jnp.sum(direction * totals), (devices, 1, LANES))
    parts = jnp.concatenate([totals.reshape(devices, chunk, LANES), term], axis=1)
    parts = jnp.sum(lax.all_to_all(parts, BOTH, 0, 0, tiled=True), axis=0)
    inner = jnp.sum(direction * direction) + parts[chunk, 0]
    step_two = norm_next / inner
    own_direction = own(direction)
    solution = step_one * right_side.reshape(chunk, LANES) + step_two * own_direction
    left_over = own(residual) - step_two * (own_direction + parts[:chunk])
    return solution.reshape(-1), left_over.reshape(-1)


def solution(mesh):
    n_row = mesh.shape["row"]
    n_col = mesh.shape["col"]
    placed = (
        P(BOTH),
        P(BOTH, None),
        P("row", "col"),
        P("row", "col"),
        P("row", "col"),
        P(),
        P(),
        P(BOTH, None, None),
        P(BOTH, None, None),
        P(BOTH, None, None),
        P(BOTH, None, None),
        P(BOTH, None),
    )
    return jax.shard_map(
        lambda *arrays: local(n_row, n_col, *arrays),
        mesh=mesh,
        in_specs=placed,
        out_specs=(P(BOTH), P(BOTH)),
        check_vma=False,
    )
```

time: 1150 us -> 319 us (0.28)
  waiting for transfers between devices: 719 us -> 147 us
  blocking collectives: 259 us -> 20.9 us
  local copies, waits for them, and re-layouts: 48.9 us -> 34.3 us
  other arithmetic: 37 us -> 24.3 us
  starting transfers between devices: 0.97 us -> 13.6 us
    reduce_scatter x4 -> x0, waiting for transfers between devices: 308 us -> none  [the longest x2 243 us: local(): lax.psum_scatter(row_terms, 'col', scatter_dimension=0, tiled=True)]
    unnamed x16 -> x3, waiting for transfers between devices: 252 us -> 1.39 us
    all_gather x2 -> x0, blocking collectives: 140 us -> none  [local(): all_duals = lax.all_gather(direction, ('row', 'col'), axis=0, tiled=True)]
    psum x3 -> x0, blocking collectives: 119 us -> none  [the longest x2 79.9 us: squared_sum(): return lax.psum(jnp.sum(vector * vector), ('row', 'col'))]
    all_gather x4 -> x1, waiting for transfers between devices: 98.9 us -> 27.8 us  [local(): lax.all_gather(jnp.concatenate([left_proj, right_proj], axis=1), BOTH, ax...]
    all_gather x1, waiting for transfers between devices: 0.02 us -> 60.3 us  [local(): basis_rows = lax.all_gather(eigen_basis, 'col', axis=0, tiled=True)]
    psum x2 -> x0, waiting for transfers between devices: 55.4 us -> none  [local(): lax.psum(own_terms.astype(jnp.bfloat16), 'row').astype(jnp.float32)]
    gather x6 -> x0, local copies, waits for them, and re-layouts: 36.1 us -> none  [the longest x4 33.1 us: local(): local_coeffs = all_duals[local_owner]]
  transfers between devices with their start and end apart: 14 -> 7, of which waited for: 11 -> 7; matrix products, arithmetic and copies ran while one was open for 8% -> 8% of each run, Pallas kernels for 0% -> 0%
where the time goes in v1:
time: 319 us; the launch traced here: 318 us
  waiting for transfers between devices  147 us (46%)
  matrix products  59.2 us (19%)
  local copies, waits for them, and re-layouts  34.3 us (11%)
  other arithmetic  24.3 us (8%)
  blocking collectives  20.9 us (7%)
  between operations  19.1 us (6%)
  starting transfers between devices  13.6 us (4%)
    all_gather x1, waiting for transfers between devices, local(): basis_rows = lax.all_gather(eigen_basis, 'col', axis=0, tiled=True)  60.3 us
    all_gather x1, waiting for transfers between devices, local(): lax.all_gather(jnp.concatenate([left_proj, right_proj], axis=1), BOTH, ax...  27.8 us
    dot_general x11, matrix products, tdot(): lax.dot_general(a, b, (((0,), (0,)), ((), ())), preferred_element_type=f32)  26.3 us
    all_gather x1, waiting for transfers between devices, local(): basis_cols = lax.all_gather(eigen_basis, 'row', axis=0, tiled=True)  23.2 us
    all_to_all x1, waiting for transfers between devices, local(): lax.all_to_all(tile_left.reshape(n_col, height, pieces), 'col', 0, 0, til...  20.5 us
    dot_general x13, matrix products, mdot(): return jnp.dot(a, b, preferred_element_type=f32)  18.4 us
    all_to_all x1, blocking collectives, local(): share = jnp.sum(lax.all_to_all(parts, BOTH, 0, 0, tiled=True), axis=0)  10.9 us
    unnamed x84, local copies, waits for them, and re-layouts  10.7 us
  transfers between devices with their start and end apart: 7, of which 7 were waited for; matrix products, arithmetic and copies ran while one was open for 8% of the time, Pallas kernels for 0%

profile of v1, /device:TPU:0, one launch (start us, length us, event | category | flops | bytes accessed | tf_op | source)
XLA Modules:
  0.0 318.1 jit_solution(17369839108127296487)
XLA Ops:
  8.7 23.2 %all-gather.6.cloned.1.call-done = bf16[1536,512]{1,0:T(8,128)(2,1)} async-done(((bf16[384,512]{1,0:T(8,128)(2,1)}), bf16[1536,512]{1,0:T(8,128)(2,1)}) %all-gather.6.cloned.1.call-update) | async-done | bytes 1572880 | tf_op jit(solution)/shard_map/all_gather | solution.py:59
  32.0 1.9 convolution_convert_fusion.2
  33.9 60.3 %all-gather.4.cloned.1.call-done = bf16[3072,512]{1,0:T(8,128)(2,1)} async-done(((bf16[384,512]{1,0:T(8,128)(2,1)}), bf16[3072,512]{1,0:T(8,128)(2,1)}) %all-gather.4.cloned.1.call-update) | async-done | bytes 3145744 | tf_op jit(solution)/shard_map/all_gather | solution.py:58
  94.2 2.5 convolution_convert_fusion.3
  98.2 3.3 %all-to-all-start = ((f32[32,9,128]{2,1,0:T(8,128)}), f32[32,9,128]{2,1,0:T(8,128)S(1)}, u32[]{:S(2)}, u32[]{:S(2)}) async-start(f32[32,9,128]{2,1,0:T(8,128)} %broadcast_in_dim.61), calls=%async_computation | async-start | bytes 524288 | tf_op jit(solution)/shard_map/all_to_all | solution.py:30
  101.5 1.9 copy.43
  103.4 2.6 copy.46
  106.1 1.8 copy.51
  107.9 1.8 convolution_convert_fusion.1
  110.2 2.7 all-to-all-done
  112.9 3.8 %all-to-all-start.2 = ((bf16[4,128,384]{1,2,0:T(8,128)(2,1)}), bf16[4,128,384]{1,2,0:T(8,128)(2,1)S(1)}, u32[]{:S(2)}, u32[]{:S(2)}) async-start(bf16[4,128,384]{1,2,0:T(8,128)(2,1)} %bitcast.175), calls=%async_computation.2 | async-start | bytes 786432 | tf_op jit(solution)/shard_map/all_to_all | solution.py:67
  118.8 1.8 fusion.65
  120.6 2.9 copy.52
  125.3 3.8 %all-to-all-start.1 = ((bf16[8,384,128]{2,1,0:T(8,128)(2,1)}), bf16[8,384,128]{2,1,0:T(8,128)(2,1)S(1)}, u32[]{:S(2)}, u32[]{:S(2)}) async-start(bf16[8,384,128]{2,1,0:T(8,128)(2,1)} %bitcast.172), calls=%async_computation.1 | async-start | bytes 1572864 | tf_op jit(solution)/shard_map/all_to_all | solution.py:64
  129.1 4.3 %fusion.23 = f32[8,256]{1,0:T(8,128)S(1)} fusion(bf16[8,256,256]{1,2,0:T(8,128)(2,1)S(1)} %convolution_convert_fusion.1, bf16[8,256,256]{2,1,0:T(8,128)(2,1)S(1)} %convolution_convert_fusion, f32[8,256,256]{2,1,0:T(8,128)} %fusion.65, f32[8,256,256]{1,2,0:T(8,128)} %copy.52, f32[8,256,256]{2,1,0:T(8,128)} %param.20, f32[8,256,256]{1,2,0:T(8,128)} %copy.51), kind=kOutput, calls=%fused_computation.36 | convolution fusion | flops 272627712 | bytes 10493952 | tf_op jit(solution)/shard_map/lpb,lba->lpa/dot_general | solution.py:131
  135.3 20.5 %all-to-all-done.1 = bf16[8,384,128]{2,1,0:T(8,128)(2,1)S(1)} async-done(((bf16[8,384,128]{2,1,0:T(8,128)(2,1)}), bf16[8,384,128]{2,1,0:T(8,128)(2,1)S(1)}, u32[]{:S(2)}, u32[]{:S(2)}) %all-to-all-start.1) | async-done | bytes 786464 | tf_op jit(solution)/shard_map/all_to_all | solution.py:64
  156.7 1.7 copy.42
  158.4 27.8 %all-gather.8.cloned.1.call-done = bf16[4096,1024]{1,0:T(8,128)(2,1)} async-done(((bf16[128,1024]{1,0:T(8,128)(2,1)}), bf16[4096,1024]{1,0:T(8,128)(2,1)}) %all-gather.8.cloned.1.call-update) | async-done | bytes 8388624 | tf_op jit(solution)/shard_map/all_gather | solution.py:70
  186.2 6.9 %fusion.6 = f32[512,512]{1,0:T(8,128)} fusion(f32[4096]{0:T(1024)S(1)} %get-tuple-element.17, bf16[4096,1024]{1,0:T(8,128)(2,1)} %all-gather.8.cloned.1.call-done), kind=kOutput, calls=%fused_computation.8 | convolution fusion | flops 2153775104 | bytes 9453568 | tf_op jit(solution)/shard_map/dot_general | solution.py:13
  193.1 2.5 copy.45
  195.6 2.7 fusion.72
  198.8 3.8 %fusion.129 = (bf16[4096,512]{1,0:T(8,128)(2,1)S(1)}, bf16[4096,512]{1,0:T(8,128)(2,1)S(1)}) fusion(bf16[4096,1024]{1,0:T(8,128)(2,1)} %all-gather.8.cloned.1.call-done), kind=kLoop, calls=%fused_computation.210 | loop fusion | bytes 16777216 | tf_op jit(solution)/shard_map/slice | solution.py:74
  206.3 1.6 fusion.87
  207.9 2.0 fusion.88
  209.9 2.5 copy.66
  212.5 2.4 fusion.57
  215.2 2.1 fusion.19
  217.3 2.7 fusion.40
  220.0 1.7 fusion.11
  221.7 10.9 %all_to_all.30 = f32[32,8,128]{2,1,0:T(8,128)} all-to-all(f32[32,8,128]{2,1,0:T(8,128)S(1)} %fusion.93), channel_id=1, replica_groups=mesh['row'=4,'col'=8] {'row','col'}, dimensions={0} | all-to-all | bytes 262144 | tf_op jit(solution)/shard_map/all_to_all | solution.py:146
  234.9 10.0 %all_to_all.31 = f32[32,8,128]{2,1,0:T(8,128)S(1)} all-to-all(f32[32,8,128]{2,1,0:T(8,128)S(1)} %broadcast_in_dim.66), channel_id=1, replica_groups=mesh['row'=4,'col'=8] {'row','col'}, dimensions={0} | all-to-all | bytes 262144 | tf_op jit(solution)/shard_map/all_to_all | solution.py:30
  250.4 1.6 reduce-precision_convert_fusion.6
  252.6 2.6 fusion.2
  255.9 1.6 multiply_convert_fusion
  258.9 3.5 %fusion.4 = f32[512,512]{1,0:T(8,128)} fusion(f32[4096]{0:T(1024)S(1)} %get-tuple-element.15, bf16[4096,1024]{1,0:T(8,128)(2,1)S(1)} %bitcast.166), kind=kOutput, calls=%fused_computation.7 | convolution fusion | flops 2153775104 | bytes 9453568 | tf_op jit(solution)/shard_map/dot_general | solution.py:13
  262.3 2.5 copy.54
  264.9 2.7 fusion.69
  268.7 2.1 fusion.56
  272.8 2.0 fusion.90
  274.8 2.3 fusion.58
  277.1 1.8 fusion.63
  278.9 2.9 copy.57
  281.8 4.4 %fusion.25 = f32[8,256]{1,0:T(8,128)S(1)} fusion(bf16[8,256,256]{1,2,0:T(8,128)(2,1)S(1)} %convolution_convert_fusion.1, bf16[8,256,256]{2,1,0:T(8,128)(2,1)S(1)} %convolution_convert_fusion, f32[8,256,256]{2,1,0:T(8,128)} %fusion.63, f32[8,256,256]{1,2,0:T(8,128)} %copy.57, f32[8,256,256]{2,1,0:T(8,128)} %param.20, f32[8,256,256]{1,2,0:T(8,128)} %copy.51), kind=kOutput, calls=%fused_computation.38 | convolution fusion | flops 272627712 | bytes 10493952 | tf_op jit(solution)/shard_map/lpb,lba->lpa/dot_general | solution.py:131
  286.2 2.1 fusion.21
  288.3 2.7 fusion.38
  291.1 1.7 fusion.10
  294.8 2.6 all-to-all-start.5
  298.0 9.8 %all-to-all-done.5 = f32[32,9,128]{2,1,0:T(8,128)S(1)} async-done(((f32[32,9,128]{2,1,0:T(8,128)}), f32[32,9,128]{2,1,0:T(8,128)S(1)}, u32[]{:S(2)}, u32[]{:S(2)}) %all-to-all-start.5) | async-done | bytes 147488 | tf_op jit(solution)/shard_map/all_to_all | solution.py:155
  (145 shorter events, 29.9 us)
Async XLA Ops:
  7.2 100.7 %copy-start = (bf16[8,256,256]{2,1,0:T(8,128)(2,1)S(1)}, bf16[8,256,256]{2,1,0:T(8,128)(2,1)}, u32[]{:S(2)}) copy-start(bf16[8,256,256]{2,1,0:T(8,128)(2,1)} %param.19) | copy-start | bytes 3145732
  7.2 87.0 %copy-start.19 = (bf16[3072,128]{1,0:T(8,128)(2,1)S(1)}, bf16[3072,128]{1,0:T(8,128)(2,1)}, u32[]{:S(2)}) copy-start(bf16[3072,128]{1,0:T(8,128)(2,1)} %param.14) | copy-start | bytes 2359300
  7.2 24.8 %all-gather.6.cloned.1.call-start = ((), (), s32[]{:S(2)}) async-start(), calls=%async_computation.7 | async-start | bytes 1966080 | tf_op jit(solution)/shard_map/all_gather | solution.py:59
  7.9 86.2 %all-gather.4.cloned.1.call-start = ((), (), s32[]{:S(2)}) async-start(), calls=%async_computation.6 | async-start | bytes 3538944 | tf_op jit(solution)/shard_map/all_gather | solution.py:58
  8.7 177.5 %all-gather.8.cloned.1.call-start = ((), (), s32[]{:S(2)}) async-start(), calls=%async_computation.8 | async-start | bytes 8650752 | tf_op jit(solution)/shard_map/all_gather | solution.py:70
  33.9 63.6 %copy-start.36 = (s32[1,128]{1,0:T(1,128)S(1)}, s32[1,128]{1,0:T(1,128)}, u32[]{:S(2)}) copy-start(s32[1,128]{1,0:T(1,128)} %param.16) | copy-start | bytes 1540
  33.9 63.6 %copy-start.31 = (f32[1024]{0:T(1024)S(1)}, f32[1024]{0:T(1024)}, u32[]{:S(2)}) copy-start(f32[1024]{0:T(1024)} %param.12) | copy-start | bytes 12292
  96.7 6.7 %copy-start.35 = (s32[8,256]{1,0:T(8,128)S(1)}, s32[8,256]{1,0:T(8,128)}, u32[]{:S(2)}) copy-start(s32[8,256]{1,0:T(8,128)} %param.23) | copy-start | bytes 24580
  97.4 8.6 %copy-start.6 = (f32[8,256,256]{2,1,0:T(8,128)S(1)}, f32[8,256,256]{2,1,0:T(8,128)}, u32[]{:S(2)}) copy-start(f32[8,256,256]{2,1,0:T(8,128)} %param.20) | copy-start | bytes 6291460
  98.2 14.7 %all-to-all-start = ((f32[32,9,128]{2,1,0:T(8,128)}), f32[32,9,128]{2,1,0:T(8,128)S(1)}, u32[]{:S(2)}, u32[]{:S(2)}) async-start(f32[32,9,128]{2,1,0:T(8,128)} %broadcast_in_dim.61), calls=%async_computation | async-start | bytes 524288 | tf_op jit(solution)/shard_map/all_to_all | solution.py:30
  107.9 1.8 copy-start.23
  112.9 5.3 %copy-start.13 = (f32[32,9,128]{2,1,0:T(8,128)}, f32[32,9,128]{2,1,0:T(8,128)S(1)}, u32[]{:S(2)}) copy-start(f32[32,9,128]{2,1,0:T(8,128)S(1)} %all-to-all-done) | copy-start | bytes 442372
  112.9 11.6 %all-to-all-start.2 = ((bf16[4,128,384]{1,2,0:T(8,128)(2,1)}), bf16[4,128,384]{1,2,0:T(8,128)(2,1)S(1)}, u32[]{:S(2)}, u32[]{:S(2)}) async-start(bf16[4,128,384]{1,2,0:T(8,128)(2,1)} %bitcast.175), calls=%async_computation.2 | async-start | bytes 786432 | tf_op jit(solution)/shard_map/all_to_all | solution.py:67
  116.7 1.4 copy-start.25
  116.7 1.4 copy-start.26
  124.5 0.8 copy-start.20
  125.3 30.5 %all-to-all-start.1 = ((bf16[8,384,128]{2,1,0:T(8,128)(2,1)}), bf16[8,384,128]{2,1,0:T(8,128)(2,1)S(1)}, u32[]{:S(2)}, u32[]{:S(2)}) async-start(bf16[8,384,128]{2,1,0:T(8,128)(2,1)} %bitcast.172), calls=%async_computation.1 | async-start | bytes 1572864 | tf_op jit(solution)/shard_map/all_to_all | solution.py:64
  155.8 0.9 copy-start.18
  193.1 2.5 copy-start.33
  195.6 2.7 copy-start.7
  202.6 2.3 copy-start.9
  202.6 5.3 %copy-start.12 = (bf16[4096,512]{1,0:T(8,128)(2,1)}, bf16[4096,512]{1,0:T(8,128)(2,1)S(1)}, u32[]{:S(2)}) copy-start(bf16[4096,512]{1,0:T(8,128)(2,1)S(1)} %get-tuple-element.8) | copy-start | bytes 12582916
  206.3 3.6 %copy-start.4 = (f32[384,512]{0,1:T(8,128)}, f32[384,512]{0,1:T(8,128)S(1)}, u32[]{:S(2)}) copy-start(f32[384,512]{0,1:T(8,128)S(1)} %fusion.48) | copy-start | bytes 2359300
  212.5 2.4 copy-start.5
  212.5 2.7 copy-start.11
  215.2 4.8 %copy-start.29 = (s32[3584]{0:T(1024)S(1)}, s32[3584]{0:T(1024)}, u32[]{:S(2)}) copy-start(s32[3584]{0:T(1024)} %get-tuple-element.27) | copy-start | bytes 43012
  220.0 25.5 %copy-start.14 = (f32[32,9,128]{2,1,0:T(8,128)S(1)}, f32[32,9,128]{2,1,0:T(8,128)}, u32[]{:S(2)}) copy-start(f32[32,9,128]{2,1,0:T(8,128)} %copy-done.13) | copy-start | bytes 442372
  244.8 0.7 copy-start.16
  252.0 0.6 copy-start.21
  252.6 2.6 copy-start.27
  252.6 6.3 %slice-start = ((s8[8388608]{0:T(1024)(128)(4,1)}), s8[4194304]{0:T(1024)(128)(4,1)S(1)}, s32[]{:S(2)}) async-start(s8[8388608]{0:T(1024)(128)(4,1)} %bitcast.165), calls=%async_computation.9 | async-start | bytes 8388608
  255.2 3.7 %slice-start.1 = ((s8[8388608]{0:T(1024)(128)(4,1)}), s8[4194304]{0:T(1024)(128)(4,1)S(1)}, s32[]{:S(2)}) async-start(s8[8388608]{0:T(1024)(128)(4,1)} %bitcast.165), calls=%async_computation.10 | async-start | bytes 8388608
  255.8 6.5 %copy-start.28 = (f32[6144]{0:T(1024)}, f32[6144]{0:T(1024)S(1)}, u32[]{:S(2)}) copy-start(f32[6144]{0:T(1024)S(1)} %fusion.13) | copy-start | bytes 73732
  262.3 2.5 copy-start.34
  264.9 2.7 copy-start.8
  267.6 1.1 copy-start.24
  271.3 1.5 copy-start.2
  272.8 2.0 slice-start.2
  281.8 4.4 %copy-start.3 = (f32[384,512]{0,1:T(8,128)S(1)}, f32[384,512]{0,1:T(8,128)}, u32[]{:S(2)}) copy-start(f32[384,512]{0,1:T(8,128)} %copy-done.2) | copy-start | bytes 2359300
  281.8 4.4 %copy-start.10 = (f32[512,1024]{0,1:T(8,128)S(1)}, f32[512,1024]{0,1:T(8,128)}, u32[]{:S(2)}) copy-start(f32[512,1024]{0,1:T(8,128)} %fusion.90) | copy-start | bytes 6291460
  286.2 4.8 %copy-start.30 = (s32[3584]{0:T(1024)S(1)}, s32[3584]{0:T(1024)}, u32[]{:S(2)}) copy-start(s32[3584]{0:T(1024)} %get-tuple-element.27) | copy-start | bytes 43012
  291.0 1.7 copy-start.22
  291.0 6.3 %copy-start.15 = (f32[32,9,128]{2,1,0:T(8,128)S(1)}, f32[32,9,128]{2,1,0:T(8,128)}, u32[]{:S(2)}) copy-start(f32[32,9,128]{2,1,0:T(8,128)} %copy-done.13) | copy-start | bytes 442372
  291.0 6.3 %copy-start.17 = (f32[32,8,128]{2,1,0:T(8,128)S(1)}, f32[32,8,128]{2,1,0:T(8,128)}, u32[]{:S(2)}) copy-start(f32[32,8,128]{2,1,0:T(8,128)} %copy-done.16) | copy-start | bytes 393220
  291.0 19.2 %copy-start.32 = (f32[1024]{0:T(1024)S(1)}, f32[1024]{0:T(1024)}, u32[]{:S(2)}) copy-start(f32[1024]{0:T(1024)} %param.12) | copy-start | bytes 12292
  291.1 20.5 %copy-start.1 = (bf16[8,256,256]{2,1,0:T(8,128)(2,1)S(1)}, bf16[8,256,256]{2,1,0:T(8,128)(2,1)}, u32[]{:S(2)}) copy-start(bf16[8,256,256]{2,1,0:T(8,128)(2,1)} %param.19) | copy-start | bytes 3145732
  294.8 13.0 %all-to-all-start.5 = ((f32[32,9,128]{2,1,0:T(8,128)}), f32[32,9,128]{2,1,0:T(8,128)S(1)}, u32[]{:S(2)}, u32[]{:S(2)}) async-start(f32[32,9,128]{2,1,0:T(8,128)} %concatenate.121), calls=%async_computation.5 | async-start | bytes 524288 | tf_op jit(solution)/shard_map/all_to_all | solution.py:155
Sparse Core Ops, SparseCore 0:
  9.6 22.3 all-gather.5
  34.1 59.9 all-gather.3
  97.6 88.5 all-gather.7

commit v2 on v1

v2 whole, which is shorter than its diff:
```python
import functools

import jax
import jax.numpy as jnp
from jax import lax
from jax.experimental import pallas as pl
from jax.experimental.pallas import tpu as pltpu
from jax.sharding import PartitionSpec as P


LANES = 128
SUB = 8
BOTH = ("row", "col")
f32 = jnp.float32
bf16 = jnp.bfloat16
VMEM_LIMIT = 56 * 1024 * 1024


def tdot(a, b):
    return lax.dot_general(a, b, (((0,), (0,)), ((), ())), preferred_element_type=f32)


def mdot(a, b):
    return jnp.dot(a, b, preferred_element_type=f32)


def exchange(x, axes):
    return lax.all_to_all(x, axes, 0, 0, tiled=True)


def spread(x, axes, size):
    return exchange(jnp.broadcast_to(x[None], (size,) + x.shape), axes)


def swap(x, axis, size, mask):
    return lax.ppermute(x, axis, [(i, i ^ mask) for i in range(size)])


def shift(x, axis, size, step):
    return lax.ppermute(x, axis, [(i, (i + step) % size) for i in range(size)])


def total(x):
    return jnp.sum(jnp.sum(x, axis=1, keepdims=True), axis=0, keepdims=True)


def halves(x):
    top = x.astype(bf16)
    return jnp.concatenate([top, (x - top.astype(f32)).astype(bf16)], axis=1)


def pick(vector, heads, lanes):
    rows = mdot(heads, halves(vector))
    rows = rows[:, :LANES] + rows[:, LANES:]
    return jnp.sum(rows * lanes.astype(f32), axis=1, keepdims=True)


def drop(values, heads_t, lanes):
    sums = mdot(heads_t, halves(values * lanes.astype(f32)))
    return sums[:, :LANES] + sums[:, LANES:]


def wide(spots, ref):
    return jnp.concatenate([ref[spots[j]] for j in range(ref.shape[0])], axis=1)


def stacked(refs):
    return jnp.concatenate([ref[...] for ref in refs], axis=0)


def curve(vector, heads, lanes, left_row, left_pair, right_row, right_pair, k_out):
    coeffs = pick(vector, heads[...], lanes[...])
    rank = left_row.shape[2]
    half = rank // 2
    grams = jnp.zeros((rank, rank), f32)
    count = heads.shape[0] // 2
    for n, (left, right) in enumerate(((left_row, right_row), (left_pair, right_pair))):
        part = coeffs[n * count : (n + 1) * count]
        scaled = (part * right[...].reshape(count, rank).astype(f32)).astype(bf16)
        grams = grams + tdot(left[...].reshape(count, rank), scaled)
    cross = grams[:half, half:] + grams[half:, :half].T
    first, last = grams[:half, :half], grams[half:, half:]
    blocks = jnp.concatenate([first + first.T, cross, last + last.T], axis=1).astype(bf16)
    for n in range(blocks.shape[1] // LANES):
        k_out[n * half : (n + 1) * half, :] = blocks[:, n * LANES : (n + 1) * LANES]


def curve_first(vector, *refs):
    curve(vector[...], *refs)


def curve_second(right, totals, *refs):
    *rest, k_out, direction_out, residual_out, steps_out = refs
    first = right[...]
    applied = first + totals[...]
    norm_now = total(first * first)
    step = norm_now / total(first * applied)
    residual = first - step * applied
    norm_next = total(residual * residual)
    direction = residual + norm_next / norm_now * first
    direction_out[...] = direction
    residual_out[...] = residual
    steps_out[0:1, :] = jnp.broadcast_to(step, (1, LANES))
    steps_out[1:2, :] = jnp.broadcast_to(norm_next, (1, LANES))
    steps_out[2:3, :] = jnp.broadcast_to(total(direction * direction), (1, LANES))
    steps_out[3:, :] = jnp.zeros((SUB - 3, LANES), f32)
    curve(direction, *rest, k_out)


def front(spots, vector, heads, lanes, group_right, u_block, v_block, *refs):
    *group_left, s_out = refs
    coeffs = pick(vector[...], heads[...], lanes[...])
    count, rank = heads.shape[0], group_right.shape[2]
    count = count - len(group_left) * group_left[0].shape[0]
    right = group_right[...].reshape(count, rank).astype(f32)
    left = stacked(group_left).astype(f32)
    field = mdot(wide(spots, u_block), (coeffs[:count] * right).astype(bf16))
    field = field + mdot(v_block[...], (coeffs[count:] * left).astype(bf16))
    s_out[...] = field.astype(bf16)


def right_project(own_right, *refs):
    *sides, out, v_out = refs
    rank = out.shape[1]
    out[...] = tdot(
        own_right[...].reshape(-1, own_right.shape[2]),
        jnp.concatenate([ref[:, :rank] for ref in sides], axis=0),
    ).astype(bf16)
    v_out[...] = jnp.concatenate([ref[:, rank:] for ref in sides], axis=1)


def left_project(order, basis, u_block, far, near):
    count = far.shape[0]
    for out, base in ((far, 0), (near, count)):
        factors = jnp.concatenate([u_block[order[base + n]] for n in range(count)], axis=1)
        out[...] = tdot(factors, basis[...]).astype(out.dtype).reshape(out.shape)


def block_values(n, vector, heads, lanes, left, right, weights):
    count = left.shape[0]
    rows = slice(n * count, (n + 1) * count)
    coeffs = pick(vector[...], heads[rows, :], lanes[rows, :])
    scaled = (coeffs * left.astype(f32)).astype(bf16)
    half_t = tdot(scaled, right)
    bent = (weights * (half_t + half_t.T)).astype(bf16)
    mixed = mdot(right, bent)
    return 2.0 * jnp.sum(left.astype(f32) * mixed, axis=1, keepdims=True)


def gather_sums(values, heads_t, lanes, out):
    sums = drop(jnp.concatenate(values, axis=0), heads_t[...], lanes[...])
    at = pl.program_id(0)

    @pl.when(at == 0)
    def _():
        out[...] = sums

    @pl.when(at > 0)
    def _():
        out[...] += sums


def blocks_ready(basis, left, right, omega, left_out, right_out, weights_out):
    for n in range(left.shape[0]):
        left_out[n] = mdot(left[n], basis[n]).astype(bf16)
        right_out[n] = mdot(right[n], basis[n]).astype(bf16)
        weights_out[n] = 0.5 * (omega[n] + omega[n].T)


def blocks_step(vector, heads, lanes, heads_t, left, right, weights, out):
    values = [
        block_values(n, vector, heads, lanes, left[n], right[n], weights[n])
        for n in range(left.shape[0])
    ]
    gather_sums(values, heads_t, lanes, out)


def back(spots, field, k_own, k_other, bend, damping, basis, heads_t, lanes, local_sums,
         group_right, u_block, v_block, *group_left):
    rank = basis.shape[1]
    half = rank // 2
    width = rank // LANES
    curvature = k_own[...].astype(f32) + k_other[...].astype(f32)
    parts = [curvature[n * half : (n + 1) * half, :] for n in range(width + width // 2)]
    top = jnp.concatenate(parts[:width], axis=1)
    low = jnp.concatenate([top[:, half:].T] + parts[width:], axis=1)
    curvature = jnp.concatenate([top, low], axis=0)
    bent = (curvature * bend[...]).astype(bf16)
    pull = field[...].astype(f32) * damping[...] - mdot(basis[...], bent)
    pull = pull.astype(bf16)
    right = group_right[...].reshape(-1, rank).astype(f32)
    back_u = tdot(wide(spots, u_block), pull) * right
    back_v = tdot(v_block[...], pull) * stacked(group_left).astype(f32)
    values_u = jnp.sum(back_u, axis=1, keepdims=True)
    values_v = jnp.sum(back_v, axis=1, keepdims=True)
    values = 2.0 * jnp.concatenate([values_u, values_v], axis=0)
    return local_sums[...] + drop(values, heads_t[...], lanes[...])


def back_first(*refs):
    *rest, out = refs
    out[...] = back(*rest)


def back_second(spots, direction, *refs):
    *rest, out = refs
    sums = back(spots, *rest)
    devices, rows, _ = out.shape
    out[:, : rows - SUB, :] = sums.reshape(devices, rows - SUB, LANES)
    term = total(direction[...] * sums)
    out[:, rows - SUB :, :] = jnp.broadcast_to(term.reshape(1, 1, 1), (devices, SUB, LANES))


def finish(at, parts, direction, residual, right_own, steps, answer, left_over):
    chunk = right_own.shape[0]
    sums = jnp.sum(parts[...], axis=0)
    step_two = steps[1:2, :] / (steps[2:3, :] + sums[chunk : chunk + 1, :])
    rows = pl.ds(at[0] * chunk, chunk)
    way = direction[rows, :]
    answer[...] = steps[0:1, :] * right_own[...] + step_two * way
    left_over[...] = residual[rows, :] - step_two * (way + sums[:chunk])


def kernel(body, outs, count, order=False):
    specs = [pl.BlockSpec(memory_space=pltpu.VMEM)] * count
    if order:
        specs = [pl.BlockSpec(memory_space=pltpu.SMEM)] + specs
    return pl.pallas_call(
        body,
        in_specs=specs,
        out_shape=outs,
        compiler_params=pltpu.CompilerParams(vmem_limit_bytes=VMEM_LIMIT),
    )


def blocks_kernel(heads, pieces, side, count, ready):
    batch = 2 if count % 2 == 0 else 1
    whole = pl.BlockSpec((heads, LANES), lambda l: (0, 0))
    square = pl.BlockSpec((batch, side, side), lambda l: (l, 0, 0))
    factor = pl.BlockSpec((batch, pieces, side), lambda l: (l, 0, 0))
    if ready:
        body = blocks_ready
        specs = [square, factor, factor, square]
        outs = (
            jax.ShapeDtypeStruct((count, pieces, side), bf16),
            jax.ShapeDtypeStruct((count, pieces, side), bf16),
            jax.ShapeDtypeStruct((count, side, side), f32),
        )
        out_specs = (factor, factor, square)
    else:
        body = blocks_step
        specs = [
            whole,
            pl.BlockSpec((batch * pieces, heads), lambda l: (l, 0)),
            pl.BlockSpec((batch * pieces, LANES), lambda l: (l, 0)),
            pl.BlockSpec((heads, batch * pieces), lambda l: (0, l)),
            factor,
            factor,
            square,
        ]
        outs, out_specs = jax.ShapeDtypeStruct((heads, LANES), f32), whole
    return pl.pallas_call(
        body,
        grid=(count // batch,),
        in_specs=specs,
        out_specs=out_specs,
        out_shape=outs,
        compiler_params=pltpu.CompilerParams(vmem_limit_bytes=VMEM_LIMIT),
    )


def local(
    n_row,
    n_col,
    right_side,
    eigen_basis,
    tile_left,
    tile_right,
    piece_owner,
    omega_main,
    damping,
    local_basis,
    local_omega,
    local_left,
    local_right,
    local_owner,
):
    devices = n_row * n_col
    pieces = tile_left.shape[1]
    height, rank = eigen_basis.shape
    chunk = right_side.shape[0] // LANES
    heads = chunk * devices
    side = local_basis.shape[1]
    blocks, local_pieces = local_owner.shape
    row_at = lax.axis_index("row")
    col_at = lax.axis_index("col")
    at = row_at * n_col + col_at
    shape = jax.ShapeDtypeStruct

    def run(body, outs, *arrays):
        return kernel(body, outs, len(arrays))(*arrays)

    def run_ordered(body, outs, *arrays):
        return kernel(body, outs, len(arrays), True)(spots, *arrays)

    own_words = jnp.concatenate(
        [right_side.reshape(chunk, LANES), piece_owner.reshape(-1, LANES).astype(f32)], axis=0
    )
    turned = jnp.transpose(tile_right.reshape(pieces, n_row, height), (1, 2, 0))
    own_right = [
        lax.dynamic_index_in_dim(turned, row_at ^ m, 0, keepdims=False) for m in range(n_row)
    ]
    sides = [jnp.concatenate([eigen_basis, part], axis=1) for part in own_right]
    sides = sides[:1] + [swap(sides[m], "row", n_row, m) for m in range(1, n_row)]
    u_block = exchange(tile_left.reshape(n_col, height, pieces), "col")

    locals_ready = blocks_kernel(heads, local_pieces, side, blocks, True)(
        local_basis, local_left, local_right, local_omega
    )
    own_words, u_block, locals_ready = lax.optimization_barrier((own_words, u_block, locals_ready))
    words = spread(own_words, BOTH, devices)
    lines = n_col // 2
    line_at, odd = col_at // 2, col_at % 2
    half_shape = (lines, pieces, rank)
    aims = 2 * jnp.arange(lines, dtype=jnp.int32)
    far, near = kernel(
        left_project, (shape(half_shape, bf16), shape(half_shape, f32)), 2, True
    )(jnp.concatenate([aims + 1 - odd, aims + odd]), eigen_basis, u_block)
    sides[1], far = lax.optimization_barrier((sides[1], far))
    right_proj, v_block = run(
        right_project,
        (shape((pieces, rank), bf16), shape((height, n_row * pieces), bf16)),
        jnp.stack(own_right), *sides,
    )
    far = swap(far, "col", n_col, 1)
    line = [right_proj] + [shift(right_proj, "col", n_col, 2 * k) for k in range(1, lines)]
    far, line = lax.optimization_barrier((far, line))
    line = jnp.stack(line)
    across = swap(line, "col", n_col, 1)

    def near_sum(k):
        at_line = (line_at + k) % lines
        here = lax.dynamic_index_in_dim(near, at_line, 0, keepdims=False)
        return here + lax.dynamic_index_in_dim(far, at_line, 0, keepdims=False).astype(f32)

    terms = [shift(near_sum(k).astype(bf16), "col", n_col, 2 * k) for k in range(1, lines)]
    terms, across = lax.optimization_barrier((terms, across))
    left_proj = near_sum(0)
    for term in terms:
        left_proj = left_proj + term.astype(f32)
    left_proj = left_proj.astype(bf16)
    right_row = jnp.concatenate([line, across], axis=0)
    group_left = [left_proj] + [swap(left_proj, "row", n_row, m) for m in range(1, n_row)]
    left_line = [left_proj] + [
        shift(left_proj, "col", n_col, 2 * k) for k in range(1, lines)
    ]
    left_row = jnp.stack(left_line + [swap(part, "col", n_col, 1) for part in left_line])
    left_pair, right_pair = swap(left_row, "row", n_row, 1), swap(right_row, "row", n_row, 1)
    steps = jnp.arange(n_col, dtype=jnp.int32)
    spots = 2 * ((line_at - steps % lines) % lines) + (odd + steps // lines) % 2
    spots = spots.astype(jnp.int32)

    right_full = words[:, :chunk].reshape(heads, LANES)
    owners_all = words[:, chunk:].astype(jnp.int32).reshape(n_row, n_col, pieces)
    owners_row = jnp.take(owners_all[row_at], spots, axis=0).reshape(-1)
    owners_pair = jnp.take(owners_all[row_at ^ 1], spots, axis=0).reshape(-1)
    owners = jnp.concatenate([owners_row] + [owners_all[row_at ^ m, col_at] for m in range(n_row)])
    owners_k = jnp.concatenate([owners_row, owners_pair])

    def table(index, size):
        return (index[:, None] == jnp.arange(size, dtype=jnp.int32)[None, :]).astype(bf16)

    def table_t(index, size):
        return (jnp.arange(size, dtype=jnp.int32)[:, None] == index[None, :]).astype(bf16)

    local_flat = local_owner.reshape(-1)
    k_heads, k_lanes = table(owners_k // LANES, heads), table(owners_k % LANES, LANES)
    tile_heads, tile_lanes = table(owners // LANES, heads), table(owners % LANES, LANES)
    tile_heads_t = table_t(owners // LANES, heads)
    block_heads, block_lanes = table(local_flat // LANES, heads), table(local_flat % LANES, LANES)
    block_heads_t = table_t(local_flat // LANES, heads)

    weight = damping.reshape(1, rank)
    bend = weight - 0.25 * (omega_main + omega_main.T)

    def blocked(vector):
        return blocks_kernel(heads, local_pieces, side, blocks, False)(
            vector, block_heads, block_lanes, block_heads_t, *locals_ready
        )

    k_rows = 3 * (rank // 2) * (rank // 2) // LANES
    k_shape = shape((k_rows, LANES), bf16)
    full_shape = shape((heads, LANES), f32)
    curve_rest = (k_heads, k_lanes, left_row, left_pair, right_row, right_pair)
    tile_rest = (right_row, u_block, v_block, *group_left)

    def fronted(vector):
        return run_ordered(
            front, shape((height, rank), bf16), vector, tile_heads, tile_lanes, *tile_rest
        )

    def back_args(field, k_part, sums):
        k_other = swap(k_part, "row", n_row, 2)
        return (field, k_part, k_other, bend, weight, eigen_basis, tile_heads_t, tile_lanes, sums, *tile_rest)

    sums = blocked(right_full)
    k_part = run(curve_first, k_shape, right_full, *curve_rest)
    parts = run_ordered(back_first, full_shape, *back_args(fronted(right_full), k_part, sums))
    share = jnp.sum(exchange(parts.reshape(devices, chunk, LANES), BOTH), axis=0)
    totals = spread(share, BOTH, devices).reshape(heads, LANES)
    k_part, direction, residual, steps = run(
        curve_second,
        (k_shape, full_shape, full_shape, shape((SUB, LANES), f32)),
        right_full, totals, *curve_rest,
    )
    sums = blocked(direction)
    parts = run_ordered(
        back_second,
        shape((devices, chunk + SUB, LANES), f32),
        direction, *back_args(fronted(direction), k_part, sums),
    )
    own_shape = shape((chunk, LANES), f32)
    answer, left_over = kernel(finish, (own_shape, own_shape), 5, True)(
        jnp.full((1,), at, jnp.int32),
        exchange(parts, BOTH), direction, residual, right_side.reshape(chunk, LANES), steps,
    )
    return answer.reshape(-1), left_over.reshape(-1)


def solution(mesh):
    placed = (
        P(BOTH),
        P(BOTH, None),
        P("row", "col"),
        P("row", "col"),
        P("row", "col"),
        P(),
        P(),
        P(BOTH, None, None),
        P(BOTH, None, None),
        P(BOTH, None, None),
        P(BOTH, None, None),
        P(BOTH, None),
    )
    return jax.shard_map(
        functools.partial(local, mesh.shape["row"], mesh.shape["col"]),
        mesh=mesh,
        in_specs=placed,
        out_specs=(P(BOTH), P(BOTH)),
        check_vma=False,
    )
```

time: 319 us -> 194 us (0.61)
  waiting for transfers between devices: 147 us -> 46 us
  Pallas kernels: 0 us -> 62.7 us
  matrix products: 59.2 us -> 0 us
  starting transfers between devices: 13.6 us -> 39.2 us
  local copies, waits for them, and re-layouts: 34.3 us -> 9.49 us
  between operations: 19.1 us -> 1.17 us
  other arithmetic: 24.3 us -> 14 us
    all_gather x3 -> x0, waiting for transfers between devices: 111 us -> none  [the longest x1 60.3 us: local(): basis_rows = lax.all_gather(eigen_basis, 'col', axis=0, tiled=True)]
    pallas_call x0 -> x12, Pallas kernels: none -> 62.7 us  [the longest x4 21.7 us: run_ordered(): return kernel(body, outs, len(arrays), True)(spots, *arrays)]
    dot_general x30 -> x0, matrix products: 59.2 us -> none  [the longest x11 26.3 us: tdot(): lax.dot_general(a, b, (((0,), (0,)), ((), ())), preferred_element_type=f32)]
    ppermute x0 -> x25, waiting for transfers between devices: none -> 27.4 us  [the longest x9 20.1 us: shift(): return lax.ppermute(x, axis, [(i, (i + step) % size) for i in range(size)])]
    ppermute x0 -> x25, starting transfers between devices: none -> 25.5 us  [the longest x9 12.8 us: shift(): return lax.ppermute(x, axis, [(i, (i + step) % size) for i in range(size)])]
    all_to_all x4 -> x3, waiting for transfers between devices: 34 us -> 18.6 us  [exchange(): return lax.all_to_all(x, axes, 0, 0, tiled=True)]
    dot_general x4 -> x0, local copies, waits for them, and re-layouts: 10.9 us -> none  [the longest x2 5.81 us: partial(): jnp.einsum('lpa,lpb->lab', scaled, local_rp, preferred_element_type=f32)]
    reduce_sum x8 -> x1, other arithmetic: 6.21 us -> 0.04 us  [local(): jnp.sum(exchange(parts.reshape(devices, chunk, LANES), BOTH), axis=0)]
  transfers between devices with their start and end apart: 7 -> 28, of which waited for: 7 -> 9; matrix products, arithmetic and copies ran while one was open for 8% -> 9% of each run, Pallas kernels for 0% -> 22%
where the time goes in v2:
time: 194 us; the launch traced here: 193 us
  Pallas kernels  62.7 us (32%)
  waiting for transfers between devices  46 us (24%)
  starting transfers between devices  39.2 us (20%)
  blocking collectives  20.6 us (11%)
  other arithmetic  14 us (7%)
  local copies, waits for them, and re-layouts  9.49 us (5%)
    pallas_call x4, Pallas kernels, run_ordered(): return kernel(body, outs, len(arrays), True)(spots, *arrays)  21.7 us
    all_to_all x2, blocking collectives, exchange(): return lax.all_to_all(x, axes, 0, 0, tiled=True)  20.6 us
    ppermute x9, waiting for transfers between devices, shift(): return lax.ppermute(x, axis, [(i, (i + step) % size) for i in range(size)])  20.1 us
    all_to_all x3, waiting for transfers between devices, exchange(): return lax.all_to_all(x, axes, 0, 0, tiled=True)  18.6 us
    pallas_call x2, Pallas kernels, blocked(): blocks_kernel(heads, local_pieces, side, blocks, False)  17.5 us
    all_to_all x3, starting transfers between devices, exchange(): return lax.all_to_all(x, axes, 0, 0, tiled=True)  13.8 us
    pallas_call x3, Pallas kernels, run(): return kernel(body, outs, len(arrays))(*arrays)  13.4 us
    ppermute x9, starting transfers between devices, shift(): return lax.ppermute(x, axis, [(i, (i + step) % size) for i in range(size)])  12.8 us
  transfers between devices with their start and end apart: 28, of which 9 were waited for; matrix products, arithmetic and copies ran while one was open for 9% of the time, Pallas kernels for 22%

profile of v2, /device:TPU:0, one launch (start us, length us, event | category | flops | bytes accessed | tf_op | source)
XLA Modules:
  0.0 193.2 jit_solution(2160340563449773616)
XLA Ops:
  0.6 7.4 %all-to-all-start = ((bf16[8,384,128]{2,1,0:T(8,128)(2,1)}), bf16[8,384,128]{2,1,0:T(8,128)(2,1)S(1)}, u32[]{:S(2)}, u32[]{:S(2)}) async-start(bf16[8,384,128]{2,1,0:T(8,128)(2,1)} %bitcast.105), calls=%async_computation | async-start | bytes 1572864 | tf_op jit(solution)/shard_map/all_to_all | solution.py:28
  8.1 1.2 copy.14
  9.5 1.4 pad_maximum_fusion.4
  13.2 5.4 %shard_map.131 = (bf16[8,256,256]{2,1,0:T(8,128)(2,1)}, bf16[8,256,256]{2,1,0:T(8,128)(2,1)}, f32[8,256,256]{2,1,0:T(8,128)}) custom-call(bf16[8,256,256]{2,1,0:T(8,128)(2,1)} %basis.2, bf16[8,256,256]{2,1,0:T(8,128)(2,1)} %left.1, bf16[8,256,256]{2,1,0:T(8,128)(2,1)} %right.1, f32[8,256,256]{2,1,0:T(8,128)} %omega.1), custom_call_target="tpu_custom_call" | custom-call | tf_op jit(solution)/shard_map/pallas_call | solution.py:317
  20.0 8.2 %all-to-all-done.u_block.refs_11_.refs_10_ = bf16[8,384,128]{2,1,0:T(8,128)(2,1)S(1)} async-done(((bf16[8,384,128]{2,1,0:T(8,128)(2,1)}), bf16[8,384,128]{2,1,0:T(8,128)(2,1)S(1)}, u32[]{:S(2)}, u32[]{:S(2)}) %all-to-all-start) | async-done | bytes 786464 | tf_op jit(solution)/shard_map/all_to_all | solution.py:28
  29.0 3.6 %all-to-all-start.1 = ((f32[32,9,128]{2,1,0:T(8,128)}), f32[32,9,128]{2,1,0:T(8,128)S(1)}, u32[]{:S(2)}, u32[]{:S(2)}) async-start(f32[32,9,128]{2,1,0:T(8,128)} %broadcast_in_dim.16), calls=%async_computation.1 | async-start | bytes 524288 | tf_op jit(solution)/shard_map/all_to_all | solution.py:28
  32.6 1.2 fusion.6.refs_4_.refs_3_
  33.9 3.0 %shard_map.132 = (bf16[4,128,512]{2,1,0:T(8,128)(2,1)}, f32[4,128,512]{2,1,0:T(8,128)}) custom-call(s32[8]{0:T(128)} %pad_add_fusion.1.order, bf16[384,512]{1,0:T(8,128)(2,1)} %refs_5_.1, bf16[8,384,128]{2,1,0:T(8,128)(2,1)} %copy-done.1), custom_call_target="tpu_custom_call" | custom-call | tf_op jit(solution)/shard_map/pallas_call | solution.py:326
  36.9 2.7 %shard_map.133 = (bf16[128,512]{1,0:T(8,128)(2,1)}, bf16[384,512]{1,0:T(8,128)(2,1)}) custom-call(bf16[4,384,128]{2,1,0:T(8,128)(2,1)} %pad_maximum_fusion.5.own_right, bf16[384,640]{1,0:T(8,128)(2,1)} %get-tuple-element.71.refs_0_, bf16[384,640]{1,0:T(8,128)(2,1)} %collective-permute-done.refs_1_, bf16[384,640]{1,0:T(8,128)(2,1)} %collective-permute-done.2.refs_2_, ...), custom_call_target="tpu_custom_call" | custom-call | tf_op jit(solution)/shard_map/pallas_call | solution.py:301
  39.6 3.6 %collective-permute-start.6 = (bf16[128,512]{1,0:T(8,128)(2,1)}, bf16[128,512]{1,0:T(8,128)(2,1)S(1)}, u32[]{:S(2)}, u32[]{:S(2)}) collective-permute-start(bf16[128,512]{1,0:T(8,128)(2,1)} %get-tuple-element.41), channel_id=1, source_target_pairs={{0,6},{1,7},{2,0},{3,1},{4,2},{5,3},{6,4},{7,5},{8,14},{9,15},{10,... | collective-permute-start | bytes 393224 | tf_op jit(solution)/shard_map/ppermute | solution.py:40
  43.2 1.1 collective-permute-start.4
  44.3 1.5 collective-permute-start.1
  46.5 1.0 fusion.4.refs_7_.refs_6_
  47.6 1.2 fusion.3.heads
  49.4 1.2 fusion.2.heads_t
  50.6 1.0 fusion.9.lanes.refs_8_.refs_7_
  51.7 1.2 fusion.7.refs_1_
  52.8 2.3 %collective-permute-done.5 = bf16[128,512]{1,0:T(8,128)(2,1)S(1)} collective-permute-done((bf16[128,512]{1,0:T(8,128)(2,1)}, bf16[128,512]{1,0:T(8,128)(2,1)S(1)}, u32[]{:S(2)}, u32[]{:S(2)}) %collective-permute-start.5) | collective-permute-done | bytes 131104 | tf_op jit(solution)/shard_map/ppermute | solution.py:40
  55.1 2.3 %collective-permute-done.1 = bf16[4,128,512]{2,1,0:T(8,128)(2,1)S(1)} collective-permute-done((bf16[4,128,512]{2,1,0:T(8,128)(2,1)S(1)}, bf16[4,128,512]{2,1,0:T(8,128)(2,1)S(1)}, u32[]{:S(2)}, u32[]{:S(2)}) %collective-permute-start.1) | collective-permute-done | bytes 524320 | tf_op jit(solution)/shard_map/ppermute | solution.py:36
  57.5 1.5 collective-permute-start.10
  59.2 3.1 %collective-permute-start.9 = (bf16[128,512]{1,0:T(8,128)(2,1)S(1)}, bf16[128,512]{1,0:T(8,128)(2,1)S(1)}, u32[]{:S(2)}, u32[]{:S(2)}) collective-permute-start(bf16[128,512]{1,0:T(8,128)(2,1)S(1)} %get-tuple-element.67), channel_id=1, source_target_pairs={{0,6},{1,7},{2,0},{3,1},{4,2},{5,3},{6,4},{7,5},{8,14},{9,15},{10,... | collective-permute-start | bytes 393224 | tf_op jit(solution)/shard_map/ppermute | solution.py:40
  63.4 2.7 %collective-permute-done.9 = bf16[128,512]{1,0:T(8,128)(2,1)S(1)} collective-permute-done((bf16[128,512]{1,0:T(8,128)(2,1)S(1)}, bf16[128,512]{1,0:T(8,128)(2,1)S(1)}, u32[]{:S(2)}, u32[]{:S(2)}) %collective-permute-start.9) | collective-permute-done | bytes 131104 | tf_op jit(solution)/shard_map/ppermute | solution.py:40
  66.2 6.9 %collective-permute-done.8 = bf16[128,512]{1,0:T(8,128)(2,1)S(1)} collective-permute-done((bf16[128,512]{1,0:T(8,128)(2,1)S(1)}, bf16[128,512]{1,0:T(8,128)(2,1)S(1)}, u32[]{:S(2)}, u32[]{:S(2)}) %collective-permute-start.8) | collective-permute-done | bytes 131104 | tf_op jit(solution)/shard_map/ppermute | solution.py:40
  73.8 1.3 collective-permute-start.15
  75.1 1.9 %collective-permute-start.14 = (bf16[128,512]{1,0:T(8,128)(2,1)S(1)}, bf16[128,512]{1,0:T(8,128)(2,1)S(1)}, u32[]{:S(2)}, u32[]{:S(2)}) collective-permute-start(bf16[128,512]{1,0:T(8,128)(2,1)S(1)} %get-tuple-element.62.refs_0_.refs_13_.refs_12_), channel_id=1, source_target_pairs={{0,2},{1,3},{2,4},{3,5},{4,6},{5,7},{6,0},{7,1},{8,10},{9,11},{10,... | collective-permute-start | bytes 393224 | tf_op jit(solution)/shard_map/ppermute | solution.py:40
  77.8 1.2 collective-permute-done.16
  79.5 7.0 %collective-permute-done.15 = bf16[128,512]{1,0:T(8,128)(2,1)S(1)} collective-permute-done((bf16[128,512]{1,0:T(8,128)(2,1)S(1)}, bf16[128,512]{1,0:T(8,128)(2,1)S(1)}, u32[]{:S(2)}, u32[]{:S(2)}) %collective-permute-start.15) | collective-permute-done | bytes 131104 | tf_op jit(solution)/shard_map/ppermute | solution.py:40
  87.1 1.5 collective-permute-start.18
  88.6 4.9 %collective-permute-done.18 = bf16[128,512]{1,0:T(8,128)(2,1)S(1)} collective-permute-done((bf16[128,512]{1,0:T(8,128)(2,1)S(1)}, bf16[128,512]{1,0:T(8,128)(2,1)S(1)}, u32[]{:S(2)}, u32[]{:S(2)}) %collective-permute-start.18) | collective-permute-done | bytes 131104 | tf_op jit(solution)/shard_map/ppermute | solution.py:36
  94.5 1.4 fusion.1.heads
  95.9 1.3 fusion.refs_0_
  97.2 1.5 collective-permute-start.13
  99.3 1.0 copy-done.5
  101.2 5.1 %shard_map.135.refs_2_ = bf16[1536,128]{1,0:T(8,128)(2,1)} custom-call(f32[256,128]{1,0:T(8,128)} %slice_bitcast_fusion.vector.right, bf16[2048,256]{1,0:T(8,128)(2,1)} %fusion.refs_0_, bf16[2048,128]{1,0:T(8,128)(2,1)} %fusion.7.refs_1_, bf16[8,128,512]{2,1,0:T(8,128)(2,1)} %copy-done.3, bf16[8,128,512]{2,1,0:T(8,128)(2,1)} %copy-done.6, ...), custom_call_target="tpu_custom_call" | custom-call | tf_op jit(solution)/shard_map/pallas_call | solution.py:301
  106.4 1.5 collective-permute-start.23
  107.9 1.2 fusion.8.lanes
  109.0 8.8 %shard_map.136.refs_9_ = f32[256,128]{1,0:T(8,128)} custom-call(f32[256,128]{1,0:T(8,128)} %slice_bitcast_fusion.vector.right, bf16[2048,256]{1,0:T(8,128)(2,1)} %fusion.1.heads, bf16[2048,128]{1,0:T(8,128)(2,1)} %fusion.8.lanes, bf16[256,2048]{1,0:T(8,128)(2,1)} %fusion.2.heads_t, bf16[8,256,256]{2,1,0:T(8,128)(2,1)} %get-tuple-element.52.left, ...), custom_call_target="tpu_custom_call" | custom-call | tf_op jit(solution)/shard_map/pallas_call | solution.py:387
  118.6 4.1 %shard_map.134.refs_1_ = bf16[384,512]{1,0:T(8,128)(2,1)} custom-call(s32[8]{0:T(128)} %copy-done.18, f32[256,128]{1,0:T(8,128)} %slice_bitcast_fusion.vector.right, bf16[1536,256]{1,0:T(8,128)(2,1)} %fusion.3.heads, bf16[1536,128]{1,0:T(8,128)(2,1)} %fusion.9.lanes.refs_8_.refs_7_, bf16[8,128,512]{2,1,0:T(8,128)(2,1)} %copy-done, ...), custom_call_target="tpu_custom_call" | custom-call | tf_op jit(solution)/shard_map/pallas_call | solution.py:304
  123.4 6.6 %shard_map.137 = f32[256,128]{1,0:T(8,128)} custom-call(s32[8]{0:T(128)} %copy-done.18, bf16[384,512]{1,0:T(8,128)(2,1)} %shard_map.134.refs_1_, bf16[1536,128]{1,0:T(8,128)(2,1)} %shard_map.135.refs_2_, bf16[1536,128]{1,0:T(8,128)(2,1)} %copy-done.14, f32[512,512]{1,0:T(8,128)} %fusion.6.refs_4_.refs_3_, f32[1,512]{1,0:T(1,128)} %bitcast.118, ...), custom_call_target="tpu_custom_call" | custom-call | tf_op jit(solution)/shard_map/pallas_call | solution.py:304
  130.0 10.4 %all_to_all.25 = f32[32,8,128]{2,1,0:T(8,128)S(1)} all-to-all(f32[32,8,128]{2,1,0:T(8,128)} %bitcast.107), channel_id=1, replica_groups=mesh['row'=4,'col'=8] {'row','col'}, dimensions={0} | all-to-all | bytes 262144 | tf_op jit(solution)/shard_map/all_to_all | solution.py:28
  140.5 10.2 %all_to_all.26 = f32[32,8,128]{2,1,0:T(8,128)} all-to-all(f32[32,8,128]{2,1,0:T(8,128)S(1)} %broadcast_in_dim.17), channel_id=1, replica_groups=mesh['row'=4,'col'=8] {'row','col'}, dimensions={0} | all-to-all | bytes 262144 | tf_op jit(solution)/shard_map/all_to_all | solution.py:28
  150.6 5.5 %shard_map.138 = (bf16[1536,128]{1,0:T(8,128)(2,1)}, f32[256,128]{1,0:T(8,128)}, f32[256,128]{1,0:T(8,128)}, f32[8,128]{1,0:T(8,128)}) custom-call(f32[256,128]{1,0:T(8,128)} %slice_bitcast_fusion.vector.right, f32[256,128]{1,0:T(8,128)} %bitcast.106, bf16[2048,256]{1,0:T(8,128)(2,1)} %fusion.refs_0_, bf16[2048,128]{1,0:T(8,128)(2,1)} %fusion.7.refs_1_, ...), custom_call_target="tpu_custom_call" | custom-call | tf_op jit(solution)/shard_map/pallas_call | solution.py:301
  157.1 8.8 %shard_map.140.refs_8_ = f32[256,128]{1,0:T(8,128)} custom-call(f32[256,128]{1,0:T(8,128)} %get-tuple-element.55.vector.direction, bf16[2048,256]{1,0:T(8,128)(2,1)} %fusion.1.heads, bf16[2048,128]{1,0:T(8,128)(2,1)} %fusion.8.lanes, bf16[256,2048]{1,0:T(8,128)(2,1)} %fusion.2.heads_t, bf16[8,256,256]{2,1,0:T(8,128)(2,1)} %get-tuple-element.52.left, ...), custom_call_target="tpu_custom_call" | custom-call | tf_op jit(solution)/shard_map/pallas_call | solution.py:387
  165.9 4.1 %shard_map.139.refs_0_ = bf16[384,512]{1,0:T(8,128)(2,1)} custom-call(s32[8]{0:T(128)} %copy-done.18, f32[256,128]{1,0:T(8,128)} %get-tuple-element.55.vector.direction, bf16[1536,256]{1,0:T(8,128)(2,1)} %fusion.3.heads, bf16[1536,128]{1,0:T(8,128)(2,1)} %fusion.9.lanes.refs_8_.refs_7_, bf16[8,128,512]{2,1,0:T(8,128)(2,1)} %copy-done, ...), custom_call_target="tpu_custom_call" | custom-call | tf_op jit(solution)/shard_map/pallas_call | solution.py:304
  170.7 6.8 %shard_map.141 = f32[32,16,128]{2,1,0:T(8,128)} custom-call(s32[8]{0:T(128)} %copy-done.18, f32[256,128]{1,0:T(8,128)} %get-tuple-element.55.vector.direction, bf16[384,512]{1,0:T(8,128)(2,1)} %shard_map.139.refs_0_, bf16[1536,128]{1,0:T(8,128)(2,1)} %get-tuple-element.56.refs_1_, bf16[1536,128]{1,0:T(8,128)(2,1)} %copy-done.15, ...), custom_call_target="tpu_custom_call" | custom-call | tf_op jit(solution)/shard_map/pallas_call | solution.py:304
  177.6 2.7 %all-to-all-start.4 = ((f32[32,16,128]{2,1,0:T(8,128)}), f32[32,16,128]{2,1,0:T(8,128)S(1)}, u32[]{:S(2)}, u32[]{:S(2)}) async-start(f32[32,16,128]{2,1,0:T(8,128)} %shard_map.141), calls=%async_computation.4 | async-start | bytes 524288 | tf_op jit(solution)/shard_map/all_to_all | solution.py:28
  180.3 10.4 %all-to-all-done.4.parts = f32[32,16,128]{2,1,0:T(8,128)S(1)} async-done(((f32[32,16,128]{2,1,0:T(8,128)}), f32[32,16,128]{2,1,0:T(8,128)S(1)}, u32[]{:S(2)}, u32[]{:S(2)}) %all-to-all-start.4) | async-done | bytes 262176 | tf_op jit(solution)/shard_map/all_to_all | solution.py:28
  191.5 1.7 shard_map.142
  (119 shorter events, 16.2 us)
Async XLA Ops:
  0.6 8.8 %copy-start.2 = (bf16[384,512]{1,0:T(8,128)(2,1)S(1)}, bf16[384,512]{1,0:T(8,128)(2,1)}, u32[]{:S(2)}) copy-start(bf16[384,512]{1,0:T(8,128)(2,1)} %refs_5_.1) | copy-start | bytes 1179652
  0.6 27.6 %all-to-all-start = ((bf16[8,384,128]{2,1,0:T(8,128)(2,1)}), bf16[8,384,128]{2,1,0:T(8,128)(2,1)S(1)}, u32[]{:S(2)}, u32[]{:S(2)}) async-start(bf16[8,384,128]{2,1,0:T(8,128)(2,1)} %bitcast.105), calls=%async_computation | async-start | bytes 1572864 | tf_op jit(solution)/shard_map/all_to_all | solution.py:28
  9.3 3.5 %copy-start.21 = (s32[1,128]{1,0:T(1,128)S(1)}, s32[1,128]{1,0:T(1,128)}, u32[]{:S(2)}) copy-start(s32[1,128]{1,0:T(1,128)} %param.18) | copy-start | bytes 1540
  9.3 3.5 %copy-start.19 = (s32[8,256]{1,0:T(8,128)S(1)}, s32[8,256]{1,0:T(8,128)}, u32[]{:S(2)}) copy-start(s32[8,256]{1,0:T(8,128)} %param.25) | copy-start | bytes 24580
  9.3 3.5 %copy-start.4 = (f32[512,512]{1,0:T(8,128)S(1)}, f32[512,512]{1,0:T(8,128)}, u32[]{:S(2)}) copy-start(f32[512,512]{1,0:T(8,128)} %param.19) | copy-start | bytes 3145732
  10.9 26.0 %collective-permute-start.3 = (bf16[384,640]{1,0:T(8,128)(2,1)}, bf16[384,640]{1,0:T(8,128)(2,1)}, u32[]{:S(2)}, u32[]{:S(2)}) collective-permute-start(bf16[384,640]{1,0:T(8,128)(2,1)} %get-tuple-element.70), channel_id=1, source_target_pairs={{0,24},{8,16},{16,8},{24,0},{1,25},{9,17},{17,9},{25,1},{2,26},{10... | collective-permute-start | bytes 1474568 | tf_op jit(solution)/shard_map/ppermute | solution.py:36
  11.6 25.3 %collective-permute-start.2 = (bf16[384,640]{1,0:T(8,128)(2,1)}, bf16[384,640]{1,0:T(8,128)(2,1)}, u32[]{:S(2)}, u32[]{:S(2)}) collective-permute-start(bf16[384,640]{1,0:T(8,128)(2,1)} %get-tuple-element.72), channel_id=1, source_target_pairs={{0,16},{8,24},{16,0},{24,8},{1,17},{9,25},{17,1},{25,9},{2,18},{10... | collective-permute-start | bytes 1474568 | tf_op jit(solution)/shard_map/ppermute | solution.py:36
  12.4 24.5 %collective-permute-start = (bf16[384,640]{1,0:T(8,128)(2,1)}, bf16[384,640]{1,0:T(8,128)(2,1)}, u32[]{:S(2)}, u32[]{:S(2)}) collective-permute-start(bf16[384,640]{1,0:T(8,128)(2,1)} %get-tuple-element.73), channel_id=1, source_target_pairs={{0,8},{8,0},{16,24},{24,16},{1,9},{9,1},{17,25},{25,17},{2,10},{10... | collective-permute-start | bytes 1474568 | tf_op jit(solution)/shard_map/ppermute | solution.py:36
  13.1 5.5 %copy-start.17 = (f32[1024]{0:T(1024)S(1)}, f32[1024]{0:T(1024)}, u32[]{:S(2)}) copy-start(f32[1024]{0:T(1024)} %param.14) | copy-start | bytes 12292
  13.2 19.5 %copy-start.16 = (f32[512]{0:T(512)S(1)}, f32[512]{0:T(512)}, u32[]{:S(2)}) copy-start(f32[512]{0:T(512)} %param.20) | copy-start | bytes 6148
  18.6 15.3 %copy-start.18 = (s32[8]{0:T(128)}, s32[8]{0:T(128)S(1)}, u32[]{:S(2)}) copy-start(s32[8]{0:T(128)S(1)} %get-tuple-element.66.spots.refs_0_) | copy-start | bytes 100
  28.2 5.6 %copy-start.1 = (bf16[8,384,128]{2,1,0:T(8,128)(2,1)}, bf16[8,384,128]{2,1,0:T(8,128)(2,1)S(1)}, u32[]{:S(2)}) copy-start(bf16[8,384,128]{2,1,0:T(8,128)(2,1)S(1)} %all-to-all-done.u_block.refs_11_.refs_10_) | copy-start | bytes 2359300
  29.0 16.8 %all-to-all-start.1 = ((f32[32,9,128]{2,1,0:T(8,128)}), f32[32,9,128]{2,1,0:T(8,128)S(1)}, u32[]{:S(2)}, u32[]{:S(2)}) async-start(f32[32,9,128]{2,1,0:T(8,128)} %broadcast_in_dim.16), calls=%async_computation.1 | async-start | bytes 524288 | tf_op jit(solution)/shard_map/all_to_all | solution.py:28
  36.9 7.5 %copy-start.20 = (bf16[4,128,512]{2,1,0:T(8,128)(2,1)S(1)}, bf16[4,128,512]{2,1,0:T(8,128)(2,1)}, u32[]{:S(2)}) copy-start(bf16[4,128,512]{2,1,0:T(8,128)(2,1)} %get-tuple-element.38) | copy-start | bytes 1572868
  39.6 17.8 %copy-start.13 = (bf16[128,512]{1,0:T(8,128)(2,1)S(1)}, bf16[128,512]{1,0:T(8,128)(2,1)}, u32[]{:S(2)}) copy-start(bf16[128,512]{1,0:T(8,128)(2,1)} %get-tuple-element.41) | copy-start | bytes 393220
  39.6 13.2 %collective-permute-start.6 = (bf16[128,512]{1,0:T(8,128)(2,1)}, bf16[128,512]{1,0:T(8,128)(2,1)S(1)}, u32[]{:S(2)}, u32[]{:S(2)}) collective-permute-start(bf16[128,512]{1,0:T(8,128)(2,1)} %get-tuple-element.41), channel_id=1, source_target_pairs={{0,6},{1,7},{2,0},{3,1},{4,2},{5,3},{6,4},{7,5},{8,14},{9,15},{10,... | collective-permute-start | bytes 393224 | tf_op jit(solution)/shard_map/ppermute | solution.py:40
  43.2 11.9 %collective-permute-start.5 = (bf16[128,512]{1,0:T(8,128)(2,1)}, bf16[128,512]{1,0:T(8,128)(2,1)S(1)}, u32[]{:S(2)}, u32[]{:S(2)}) collective-permute-start(bf16[128,512]{1,0:T(8,128)(2,1)} %get-tuple-element.41), channel_id=1, source_target_pairs={{0,4},{1,5},{2,6},{3,7},{4,0},{5,1},{6,2},{7,3},{8,12},{9,13},{10,... | collective-permute-start | bytes 393224 | tf_op jit(solution)/shard_map/ppermute | solution.py:40
  43.2 11.9 %collective-permute-start.4 = (bf16[128,512]{1,0:T(8,128)(2,1)}, bf16[128,512]{1,0:T(8,128)(2,1)S(1)}, u32[]{:S(2)}, u32[]{:S(2)}) collective-permute-start(bf16[128,512]{1,0:T(8,128)(2,1)} %get-tuple-element.41), channel_id=1, source_target_pairs={{0,2},{1,3},{2,4},{3,5},{4,6},{5,7},{6,0},{7,1},{8,10},{9,11},{10,... | collective-permute-start | bytes 393224 | tf_op jit(solution)/shard_map/ppermute | solution.py:40
  44.3 13.1 %collective-permute-start.1 = (bf16[4,128,512]{2,1,0:T(8,128)(2,1)S(1)}, bf16[4,128,512]{2,1,0:T(8,128)(2,1)S(1)}, u32[]{:S(2)}, u32[]{:S(2)}) collective-permute-start(bf16[4,128,512]{2,1,0:T(8,128)(2,1)S(1)} %copy-done.20), channel_id=1, source_target_pairs={{0,1},{1,0},{2,3},{3,2},{4,5},{5,4},{6,7},{7,6},{8,9},{9,8},{10,11... | collective-permute-start | bytes 1572872 | tf_op jit(solution)/shard_map/ppermute | solution.py:36
  47.6 11.5 %copy-start.12 = (f32[4,128,512]{2,1,0:T(8,128)S(1)}, f32[4,128,512]{2,1,0:T(8,128)}, u32[]{:S(2)}) copy-start(f32[4,128,512]{2,1,0:T(8,128)} %get-tuple-element.45) | copy-start | bytes 3145732
  57.5 15.6 %collective-permute-start.10 = (bf16[4,128,512]{2,1,0:T(8,128)(2,1)S(1)}, bf16[4,128,512]{2,1,0:T(8,128)(2,1)S(1)}, u32[]{:S(2)}, u32[]{:S(2)}) collective-permute-start(bf16[4,128,512]{2,1,0:T(8,128)(2,1)S(1)} %pad_maximum_fusion), channel_id=1, source_target_pairs={{0,1},{1,0},{2,3},{3,2},{4,5},{5,4},{6,7},{7,6},{8,9},{9,8},{10,11... | collective-permute-start | bytes 1572872 | tf_op jit(solution)/shard_map/ppermute | solution.py:36
  59.2 7.0 %collective-permute-start.9 = (bf16[128,512]{1,0:T(8,128)(2,1)S(1)}, bf16[128,512]{1,0:T(8,128)(2,1)S(1)}, u32[]{:S(2)}, u32[]{:S(2)}) collective-permute-start(bf16[128,512]{1,0:T(8,128)(2,1)S(1)} %get-tuple-element.67), channel_id=1, source_target_pairs={{0,6},{1,7},{2,0},{3,1},{4,2},{5,3},{6,4},{7,5},{8,14},{9,15},{10,... | collective-permute-start | bytes 393224 | tf_op jit(solution)/shard_map/ppermute | solution.py:40
  62.3 10.8 %collective-permute-start.8 = (bf16[128,512]{1,0:T(8,128)(2,1)S(1)}, bf16[128,512]{1,0:T(8,128)(2,1)S(1)}, u32[]{:S(2)}, u32[]{:S(2)}) collective-permute-start(bf16[128,512]{1,0:T(8,128)(2,1)S(1)} %get-tuple-element.68), channel_id=1, source_target_pairs={{0,4},{1,5},{2,6},{3,7},{4,0},{5,1},{6,2},{7,3},{8,12},{9,13},{10,... | collective-permute-start | bytes 393224 | tf_op jit(solution)/shard_map/ppermute | solution.py:40
  63.1 10.0 %collective-permute-start.7 = (bf16[128,512]{1,0:T(8,128)(2,1)S(1)}, bf16[128,512]{1,0:T(8,128)(2,1)S(1)}, u32[]{:S(2)}, u32[]{:S(2)}) collective-permute-start(bf16[128,512]{1,0:T(8,128)(2,1)S(1)} %get-tuple-element.69), channel_id=1, source_target_pairs={{0,2},{1,3},{2,4},{3,5},{4,6},{5,7},{6,0},{7,1},{8,10},{9,11},{10,... | collective-permute-start | bytes 393224 | tf_op jit(solution)/shard_map/ppermute | solution.py:40
  73.2 26.0 %copy-start.7 = (bf16[128,512]{1,0:T(8,128)(2,1)}, bf16[128,512]{1,0:T(8,128)(2,1)S(1)}, u32[]{:S(2)}) copy-start(bf16[128,512]{1,0:T(8,128)(2,1)S(1)} %get-tuple-element.62.refs_0_.refs_13_.refs_12_) | copy-start | bytes 393220
  73.2 5.8 %collective-permute-start.16 = (bf16[128,512]{1,0:T(8,128)(2,1)S(1)}, bf16[128,512]{1,0:T(8,128)(2,1)S(1)}, u32[]{:S(2)}, u32[]{:S(2)}) collective-permute-start(bf16[128,512]{1,0:T(8,128)(2,1)S(1)} %get-tuple-element.62.refs_0_.refs_13_.refs_12_), channel_id=1, source_target_pairs={{0,6},{1,7},{2,0},{3,1},{4,2},{5,3},{6,4},{7,5},{8,14},{9,15},{10,... | collective-permute-start | bytes 393224 | tf_op jit(solution)/shard_map/ppermute | solution.py:40
  73.8 12.7 %collective-permute-start.15 = (bf16[128,512]{1,0:T(8,128)(2,1)S(1)}, bf16[128,512]{1,0:T(8,128)(2,1)S(1)}, u32[]{:S(2)}, u32[]{:S(2)}) collective-permute-start(bf16[128,512]{1,0:T(8,128)(2,1)S(1)} %get-tuple-element.62.refs_0_.refs_13_.refs_12_), channel_id=1, source_target_pairs={{0,4},{1,5},{2,6},{3,7},{4,0},{5,1},{6,2},{7,3},{8,12},{9,13},{10,... | collective-permute-start | bytes 393224 | tf_op jit(solution)/shard_map/ppermute | solution.py:40
  75.1 12.0 %collective-permute-start.14 = (bf16[128,512]{1,0:T(8,128)(2,1)S(1)}, bf16[128,512]{1,0:T(8,128)(2,1)S(1)}, u32[]{:S(2)}, u32[]{:S(2)}) collective-permute-start(bf16[128,512]{1,0:T(8,128)(2,1)S(1)} %get-tuple-element.62.refs_0_.refs_13_.refs_12_), channel_id=1, source_target_pairs={{0,2},{1,3},{2,4},{3,5},{4,6},{5,7},{6,0},{7,1},{8,10},{9,11},{10,... | collective-permute-start | bytes 393224 | tf_op jit(solution)/shard_map/ppermute | solution.py:40
  77.1 11.5 %collective-permute-start.17 = (bf16[128,512]{1,0:T(8,128)(2,1)S(1)}, bf16[128,512]{1,0:T(8,128)(2,1)S(1)}, u32[]{:S(2)}, u32[]{:S(2)}) collective-permute-start(bf16[128,512]{1,0:T(8,128)(2,1)S(1)} %get-tuple-element.62.refs_0_.refs_13_.refs_12_), channel_id=1, source_target_pairs={{0,1},{1,0},{2,3},{3,2},{4,5},{5,4},{6,7},{7,6},{8,9},{9,8},{10,11... | collective-permute-start | bytes 393224 | tf_op jit(solution)/shard_map/ppermute | solution.py:36
  77.7 19.4 %copy-start = (bf16[8,128,512]{2,1,0:T(8,128)(2,1)}, bf16[8,128,512]{2,1,0:T(8,128)(2,1)S(1)}, u32[]{:S(2)}) copy-start(bf16[8,128,512]{2,1,0:T(8,128)(2,1)S(1)} %constant_dynamic-update-slice_fusion.1.group_right.refs_4_.refs_10_.refs_9_) | copy-start | bytes 3145732
  77.7 21.5 %collective-permute-start.22 = (bf16[8,128,512]{2,1,0:T(8,128)(2,1)S(1)}, bf16[8,128,512]{2,1,0:T(8,128)(2,1)S(1)}, u32[]{:S(2)}, u32[]{:S(2)}) collective-permute-start(bf16[8,128,512]{2,1,0:T(8,128)(2,1)S(1)} %constant_dynamic-update-slice_fusion.1.group_right.refs_4_.refs_10_.refs_9_), channel_id=1, source_target_pairs={{0,8},{8,0},{16,24},{24,16},{1,9},{9,1},{17,25},{25,17},{2,10},{10... | collective-permute-start | bytes 3145736 | tf_op jit(solution)/shard_map/ppermute | solution.py:36
  79.0 14.6 %collective-permute-start.20 = (bf16[128,512]{1,0:T(8,128)(2,1)S(1)}, bf16[128,512]{1,0:T(8,128)(2,1)S(1)}, u32[]{:S(2)}, u32[]{:S(2)}) collective-permute-start(bf16[128,512]{1,0:T(8,128)(2,1)S(1)} %collective-permute-done.16), channel_id=1, source_target_pairs={{0,1},{1,0},{2,3},{3,2},{4,5},{5,4},{6,7},{7,6},{8,9},{9,8},{10,11... | collective-permute-start | bytes 393224 | tf_op jit(solution)/shard_map/ppermute | solution.py:36
  86.5 7.0 %collective-permute-start.19 = (bf16[128,512]{1,0:T(8,128)(2,1)S(1)}, bf16[128,512]{1,0:T(8,128)(2,1)S(1)}, u32[]{:S(2)}, u32[]{:S(2)}) collective-permute-start(bf16[128,512]{1,0:T(8,128)(2,1)S(1)} %collective-permute-done.15), channel_id=1, source_target_pairs={{0,1},{1,0},{2,3},{3,2},{4,5},{5,4},{6,7},{7,6},{8,9},{9,8},{10,11... | collective-permute-start | bytes 393224 | tf_op jit(solution)/shard_map/ppermute | solution.py:36
  87.1 6.5 %collective-permute-start.18 = (bf16[128,512]{1,0:T(8,128)(2,1)S(1)}, bf16[128,512]{1,0:T(8,128)(2,1)S(1)}, u32[]{:S(2)}, u32[]{:S(2)}) collective-permute-start(bf16[128,512]{1,0:T(8,128)(2,1)S(1)} %collective-permute-done.14), channel_id=1, source_target_pairs={{0,1},{1,0},{2,3},{3,2},{4,5},{5,4},{6,7},{7,6},{8,9},{9,8},{10,11... | collective-permute-start | bytes 393224 | tf_op jit(solution)/shard_map/ppermute | solution.py:36
  93.6 5.6 %copy-start.3 = (bf16[8,128,512]{2,1,0:T(8,128)(2,1)}, bf16[8,128,512]{2,1,0:T(8,128)(2,1)S(1)}, u32[]{:S(2)}) copy-start(bf16[8,128,512]{2,1,0:T(8,128)(2,1)S(1)} %bitcast_dynamic-update-slice_fusion.refs_2_) | copy-start | bytes 3145732
  93.6 5.6 %collective-permute-start.21 = (bf16[8,128,512]{2,1,0:T(8,128)(2,1)S(1)}, bf16[8,128,512]{2,1,0:T(8,128)(2,1)S(1)}, u32[]{:S(2)}, u32[]{:S(2)}) collective-permute-start(bf16[8,128,512]{2,1,0:T(8,128)(2,1)S(1)} %bitcast_dynamic-update-slice_fusion.refs_2_), channel_id=1, source_target_pairs={{0,8},{8,0},{16,24},{24,16},{1,9},{9,1},{17,25},{25,17},{2,10},{10... | collective-permute-start | bytes 3145736 | tf_op jit(solution)/shard_map/ppermute | solution.py:36
  97.2 20.6 %collective-permute-start.13 = (bf16[128,512]{1,0:T(8,128)(2,1)S(1)}, bf16[128,512]{1,0:T(8,128)(2,1)S(1)}, u32[]{:S(2)}, u32[]{:S(2)}) collective-permute-start(bf16[128,512]{1,0:T(8,128)(2,1)S(1)} %get-tuple-element.62.refs_0_.refs_13_.refs_12_), channel_id=1, source_target_pairs={{0,24},{8,16},{16,8},{24,0},{1,25},{9,17},{17,9},{25,1},{2,26},{10... | collective-permute-start | bytes 393224 | tf_op jit(solution)/shard_map/ppermute | solution.py:36
  98.7 19.1 %collective-permute-start.12 = (bf16[128,512]{1,0:T(8,128)(2,1)S(1)}, bf16[128,512]{1,0:T(8,128)(2,1)S(1)}, u32[]{:S(2)}, u32[]{:S(2)}) collective-permute-start(bf16[128,512]{1,0:T(8,128)(2,1)S(1)} %get-tuple-element.62.refs_0_.refs_13_.refs_12_), channel_id=1, source_target_pairs={{0,16},{8,24},{16,0},{24,8},{1,17},{9,25},{17,1},{25,9},{2,18},{10... | collective-permute-start | bytes 393224 | tf_op jit(solution)/shard_map/ppermute | solution.py:36
  99.2 18.6 %collective-permute-start.11 = (bf16[128,512]{1,0:T(8,128)(2,1)S(1)}, bf16[128,512]{1,0:T(8,128)(2,1)S(1)}, u32[]{:S(2)}, u32[]{:S(2)}) collective-permute-start(bf16[128,512]{1,0:T(8,128)(2,1)S(1)} %get-tuple-element.62.refs_0_.refs_13_.refs_12_), channel_id=1, source_target_pairs={{0,8},{8,0},{16,24},{24,16},{1,9},{9,1},{17,25},{25,17},{2,10},{10... | collective-permute-start | bytes 393224 | tf_op jit(solution)/shard_map/ppermute | solution.py:36
  99.2 1.0 copy-start.5
  100.2 1.0 copy-start.6
  106.4 16.3 %collective-permute-start.23 = (bf16[1536,128]{1,0:T(8,128)(2,1)}, bf16[1536,128]{1,0:T(8,128)(2,1)S(1)}, u32[]{:S(2)}, u32[]{:S(2)}) collective-permute-start(bf16[1536,128]{1,0:T(8,128)(2,1)} %shard_map.135.refs_2_), channel_id=1, source_target_pairs={{0,16},{8,24},{16,0},{24,8},{1,17},{9,25},{17,1},{25,9},{2,18},{10... | collective-permute-start | bytes 1179656 | tf_op jit(solution)/shard_map/ppermute | solution.py:36
  117.8 0.7 copy-start.10
  122.7 0.7 copy-start.14
  156.2 13.8 %collective-permute-start.24 = (bf16[1536,128]{1,0:T(8,128)(2,1)}, bf16[1536,128]{1,0:T(8,128)(2,1)S(1)}, u32[]{:S(2)}, u32[]{:S(2)}) collective-permute-start(bf16[1536,128]{1,0:T(8,128)(2,1)} %get-tuple-element.56.refs_1_), channel_id=1, source_target_pairs={{0,16},{8,24},{16,0},{24,8},{1,17},{9,25},{17,1},{25,9},{2,18},{10... | collective-permute-start | bytes 1179656 | tf_op jit(solution)/shard_map/ppermute | solution.py:36
  170.0 0.8 copy-start.15
  177.6 13.2 %all-to-all-start.4 = ((f32[32,16,128]{2,1,0:T(8,128)}), f32[32,16,128]{2,1,0:T(8,128)S(1)}, u32[]{:S(2)}, u32[]{:S(2)}) async-start(f32[32,16,128]{2,1,0:T(8,128)} %shard_map.141), calls=%async_computation.4 | async-start | bytes 524288 | tf_op jit(solution)/shard_map/all_to_all | solution.py:28
  190.7 0.7 copy-start.11
  (2 other events, 1.3 us)
